TPU v7x, 256 devices: a whole 4x4x8 slice. The times are simulated.
256 devices in a mesh: mem: 4 (over y), cell: 64 (over x, z, core).
Axes of the slice: x: 4, y: 4, z: 8, core: 2. Of those that a mesh axis runs over, the one named last changes fastest.
Arguments:
- depth: float32 [64, 1048576], P('mem', 'cell'), may hold values from 1 to 3
- discharge: float32 [64, 1048576], P('mem', 'cell'), may hold values from -1.5 to 1.5
- gate: int32 [1048576], P('cell'), may hold values from 0 to 1, as said below
- pump: int32 [2, 1048576], P(None, 'cell'), may hold values 0 or 1
- pump_rate: float32 [1048576], P('cell'), may hold values from 1 to 5
- obs_index: int32 [64, 512], P('cell'), may hold values from 0 to 16383, as said below
- obs_value: float32 [64, 512], P('cell'), may hold values from 1 to 3
- obs_error: float32 [64, 512], P('cell'), may hold values from 0.25 to 1.04
Outputs:
- depth_analysis: float32 [64, 1048576], P('mem', 'cell')
- discharge_analysis: float32 [64, 1048576], P('mem', 'cell')
Inputs may be any that keep to these rules, and one draw needn't show every extreme that they name: The gate on the first face of every slab after the first (cells s * 16384 with s >= 1) is open. `obs_index`: the offsets of one slab are distinct.
All inputs are finite; a program needn't handle non-finite values. No bound on the sum of `pump` on one device may be relied on, other than what follows from the above.
Results may differ from a plain program's by a relative error of at most 0.0003.
Values sent between devices are 32-bit elements; how exact they have to be, the bound alone decides.
No kernel may reach another device: no remote copies, remote signals or barrier semaphores. Data moves between devices by JAX's collectives and lax.ppermute only.
A program may use at most 64 MiB of HBM per device.

v0:
```python
import jax
import jax.numpy as jnp
from jax import lax
from jax.sharding import PartitionSpec as P

PER = 512
NS_ITERS = 12


gravity = 9.81
step_dt = 0.06


def padded_2(block, sides, width):
    for axis, dim in sides:
        count = lax.axis_size(axis)
        forward = [(i, i + 1) for i in range(count - 1)]
        backward = [(target, source) for source, target in forward]
        low = lax.ppermute(
            lax.slice_in_dim(block, block.shape[dim] - width, None, axis=dim), axis, forward
        )
        high = lax.ppermute(lax.slice_in_dim(block, 0, width, axis=dim), axis, backward)
        block = jnp.concatenate([low, block, high], axis=dim)
    return block


def from_everyone(x, axis):
    copies = jnp.broadcast_to(x, (lax.axis_size(axis), *x.shape))
    return lax.all_to_all(copies, axis, split_axis=0, concat_axis=0, tiled=True)


def taken_together(x, axis):
    everything = from_everyone(x, axis)
    return jnp.sum(everything, axis=0)


def in_one(arrays, axis):
    ends = [0]
    for a in arrays:
        ends.append(ends[-1] + a.size)
    subtotal = taken_together(jnp.concatenate([a.ravel() for a in arrays]), axis)
    return tuple((subtotal[b:e].reshape(a.shape) for a, b, e in zip(arrays, ends, ends[1:])))


def face_fluxes(depth_left, flow_left, depth_right, flow_right, faces):
    opened = faces > 0.5
    safe_dl = jnp.where(opened, depth_left, 1.0)
    safe_fl = jnp.where(opened, flow_left, 0.0)
    safe_dr = jnp.where(opened, depth_right, 1.0)
    safe_fr = jnp.where(opened, flow_right, 0.0)
    speed_left = safe_fl / safe_dl
    speed_right = safe_fr / safe_dr
    wave_left = jnp.sqrt(gravity * safe_dl)
    wave_right = jnp.sqrt(gravity * safe_dr)
    slowest = jnp.minimum(jnp.minimum(speed_left - wave_left, speed_right - wave_right), 0.0)
    fastest = jnp.maximum(jnp.maximum(speed_left + wave_left, speed_right + wave_right), 0.0)
    moment_left = safe_fl * speed_left + 0.5 * gravity * safe_dl * safe_dl
    moment_right = safe_fr * speed_right + 0.5 * gravity * safe_dr * safe_dr
    spread = fastest - slowest
    mass = (
        fastest * safe_fl - slowest * safe_fr + slowest * fastest * (safe_dr - safe_dl)
    ) / spread
    moment = (
        fastest * moment_left - slowest * moment_right + slowest * fastest * (safe_fr - safe_fl)
    ) / spread
    mass = jnp.where(opened, mass, 0.0)
    left_side = jnp.where(opened, moment, 0.5 * gravity * depth_left * depth_left)
    right_side = jnp.where(opened, moment, 0.5 * gravity * depth_right * depth_right)
    return (mass, left_side, right_side)


def advance(depth_pad, flow_pad, faces, inflow):
    mass, left_side, right_side = face_fluxes(
        depth_pad[..., :-1], flow_pad[..., :-1], depth_pad[..., 1:], flow_pad[..., 1:], faces
    )
    depth_new = depth_pad[..., 1:-1] - step_dt * (mass[..., 1:] - mass[..., :-1]) + step_dt * inflow
    flow_new = flow_pad[..., 1:-1] - step_dt * (left_side[..., 1:] - right_side[..., :-1])
    return (depth_new, flow_new)


def batch_product(first, second):
    return jnp.einsum("uij,ujk->uik", first, second, precision=lax.Precision.HIGHEST)


def transform_units(grams, cross, factor_rho):
    count = grams.shape[-1]
    identity = jnp.eye(count, dtype=jnp.float32)
    system = identity + factor_rho * factor_rho / (count - 1) * grams
    norm_scale = jnp.sqrt(jnp.sum(system * system, axis=(1, 2)))
    iterate = system / norm_scale[:, None, None]
    inverse = jnp.broadcast_to(identity, system.shape)

    def newton_step(turn, carry):
        current, invroot = carry
        factor = 1.5 * identity - 0.5 * batch_product(invroot, current)
        return (batch_product(current, factor), batch_product(factor, invroot))

    iterate, inverse = lax.fori_loop(0, NS_ITERS, newton_step, (iterate, inverse))
    root_weight = inverse / jnp.sqrt(norm_scale)[:, None, None]
    solved = batch_product(inverse, inverse) / norm_scale[:, None, None]
    mean_weight = (
        factor_rho
        / (count - 1)
        * jnp.einsum("uij,uj->ui", solved, cross, precision=lax.Precision.HIGHEST)
    )
    return factor_rho * (root_weight + mean_weight[:, :, None])


def window_sums(block_grams, block_cross):
    grams = block_grams[:-2] + block_grams[1:-1] + block_grams[2:]
    cross = block_cross[:-2] + block_cross[1:-1] + block_cross[2:]
    return (grams, cross)


def shards(depth, discharge, gate, pump, pump_rate, obs_index, obs_value, obs_error):
    member_rows = depth.shape[0]
    cell_count = depth.shape[1]
    slab_count = lax.axis_size("cell")
    quarter_count = lax.axis_size("mem")
    members = member_rows * quarter_count
    quart_cells = cell_count // quarter_count
    sub_count = quart_cells // PER
    obs_count = obs_index.shape[1]
    total_obs = obs_count * slab_count
    slab_here = lax.axis_index("cell")
    first_slab = slab_here == 0
    last_slab = slab_here == slab_count - 1
    left_open = gate.at[0].set(jnp.where(first_slab, 0, gate[0]))
    right_face = jnp.where(last_slab, 0, 1).astype(jnp.int32).reshape(1)
    faces = jnp.concatenate([left_open, right_face]).astype(jnp.float32)
    depth_now, flow_now = (depth, discharge)
    for step in range(pump.shape[0]):
        padded = padded_2(jnp.stack([depth_now, flow_now]), (("cell", 2),), 1)
        inflow = pump_rate * pump[step].astype(jnp.float32)
        depth_now, flow_now = advance(padded[0], padded[1], faces, inflow)
    offsets = obs_index[0]
    precision_obs = 1.0 / obs_error[0]
    values_obs = obs_value[0]
    value_row = jnp.zeros((cell_count,), jnp.float32).at[offsets].set(values_obs)
    prec_row = jnp.zeros((cell_count,), jnp.float32).at[offsets].set(precision_obs)
    stacked = jnp.concatenate([depth_now, value_row[None, :], prec_row[None, :]], axis=0)
    extended = padded_2(stacked, (("cell", 1),), PER)
    row_total = extended.shape[0]
    seen_local = depth_now[:, offsets]
    seen_all = lax.all_gather(seen_local, "mem", axis=0, tiled=True)
    seen_mean = jnp.mean(seen_all, axis=0)
    scaled_seen = (seen_all - seen_mean[None, :]) * precision_obs[None, :]
    innov_seen = (values_obs - seen_mean) * precision_obs
    total_misfit, total_spread = in_one(
        (jnp.sum(innov_seen * innov_seen), jnp.sum(scaled_seen * scaled_seen) / (members - 1)),
        "cell",
    )
    head = extended[:, :cell_count].reshape(row_total, quarter_count, quart_cells)[:, :, :PER]
    core = extended[:, PER : PER + cell_count].reshape(row_total, quarter_count, quart_cells)
    tail = extended[:, 2 * PER :].reshape(row_total, quarter_count, quart_cells)[
        :, :, quart_cells - PER :
    ]
    windows = jnp.concatenate([head, core, tail], axis=2)
    flow_quarters = flow_now.reshape(member_rows, quarter_count, quart_cells)
    moved_depth, moved_flow = (
        lax.all_to_all(windows[:member_rows], "mem", split_axis=1, concat_axis=0, tiled=True),
        lax.all_to_all(flow_quarters, "mem", split_axis=1, concat_axis=0, tiled=True),
    )
    window_depth = moved_depth[:, 0]
    quarter_flow = moved_flow[:, 0]
    obs_window = lax.dynamic_index_in_dim(
        windows[member_rows:], lax.axis_index("mem"), 1, keepdims=False
    )
    window_mean = jnp.mean(window_depth, axis=0)
    scaled = (window_depth - window_mean[None, :]) * obs_window[1][None, :]
    innov = (obs_window[0] - window_mean) * obs_window[1]
    blocks = scaled.reshape(members, sub_count + 2, PER)
    block_grams = jnp.einsum("ibr,jbr->bij", blocks, blocks, precision=lax.Precision.HIGHEST)
    block_cross = jnp.einsum(
        "ibr,br->bi", blocks, innov.reshape(sub_count + 2, PER), precision=lax.Precision.HIGHEST
    )
    grams, cross = window_sums(block_grams, block_cross)
    factor_rho = jnp.sqrt(total_misfit / (total_spread + total_obs))
    mixing = transform_units(grams, cross, factor_rho)
    fields = jnp.stack([window_depth[:, PER : PER + quart_cells], quarter_flow]).reshape(
        2, members, sub_count, PER
    )
    field_mean = jnp.mean(fields, axis=1, keepdims=True)
    analysed = field_mean + jnp.einsum(
        "fipr,pij->fjpr", fields - field_mean, mixing, precision=lax.Precision.HIGHEST
    )
    restored = lax.all_to_all(
        analysed.reshape(2, members, quart_cells), "mem", split_axis=1, concat_axis=2, tiled=True
    )
    return (restored[0], restored[1])


def solution(mesh):
    return jax.shard_map(
        shards,
        mesh=mesh,
        in_specs=(
            P("mem", "cell"),
            P("mem", "cell"),
            P("cell"),
            P(None, "cell"),
            P("cell"),
            P("cell", None),
            P("cell", None),
            P("cell", None),
        ),
        out_specs=(P("mem", "cell"), P("mem", "cell")),
        check_vma=False,
    )
```

profile of v0, /device:TPU:2, one launch (start us, length us, event | category | flops | bytes accessed | tf_op | source)
XLA Modules:
  0.0 209.3 jit_solution(5050971680247956712)
XLA Ops:
  0.6 0.8 copy.243
  1.5 1.0 fusion.72
  2.5 7.2 %collective-permute-start.1 = (f32[2,16,1]{2,1,0:T(8,128)S(1)}, f32[2,16,1]{2,1,0:T(8,128)S(1)}, u32[]{:S(2)}, u32[]{:S(2)}) collective-permute-start(f32[2,16,1]{2,1,0:T(8,128)S(1)} %get-tuple-element.91), channel_id=1, source_target_pairs={{1,0},{2,1},{3,2},{4,3},{5,4},{6,5},{7,6},{8,7},{9,8},{10,9},{11,1... | collective-permute-start | bytes 392 | tf_op jit(solution)/shard_map/ppermute | solution.py:22
  9.6 1.9 collective-permute-start
  11.6 1.5 pad_maximum_fusion
  14.5 2.5 %scatter_custom_fusion.1 = f32[16384]{0:T(1024)S(1)} fusion(s32[512]{0:T(512)S(1)} %bitcast.157, f32[512]{0:T(512)S(1)} %bitcast.151, f32[]{:T(128)} %constant.72.clone.1), kind=kCustom, calls=%fused_computation.138 | custom fusion | bytes 65540 | tf_op jit(solution)/shard_map/scatter | solution.py:140
  17.1 2.6 %scatter_custom_fusion = f32[16384]{0:T(1024)S(1)} fusion(s32[512]{0:T(512)S(1)} %bitcast.158, f32[512]{0:T(512)} %bitcast.159, f32[]{:T(128)} %constant.72.clone.1), kind=kCustom, calls=%fused_computation.140 | custom fusion | bytes 66048 | tf_op jit(solution)/shard_map/scatter | solution.py:139
  19.7 3.1 %concatenate.37 = f32[2,16,16386]{2,1,0:T(8,128)S(1)} concatenate(f32[2,16,1]{2,1,0:T(8,128)S(1)} %collective-permute-done, f32[2,16,16384]{2,1,0:T(8,128)} %pad_maximum_fusion, f32[2,16,1]{2,1,0:T(8,128)S(1)} %collective-permute-done.1), dimensions={2} | concatenate | bytes 4194816 | tf_op jit(solution)/shard_map/concatenate | solution.py:23
  23.0 2.2 %fusion.12 = (f32[16,16385]{1,0:T(8,128)S(1)}, f32[16,16385]{1,0:T(8,128)S(1)}, f32[16,16385]{1,0:T(8,128)S(1)}, f32[16,16385]{1,0:T(8,128)S(1)}) fusion(f32[16,16386]{1,0:T(8,128)S(1)} %get-tuple-element.86, pred[16385]{0:T(1024)(128)(4,1)S(1)} %fusion.58, f32[16,16386]{1,0:T(8,128)S(1)} %get-tuple-element.85), kind=kLoop, calls=%fused_computation.43 | loop fusion | flops 10748560 | bytes 8405505 | tf_op jit(solution)/shard_map/div | solution.py:63
  25.1 1.4 fusion.26
  26.7 5.7 %collective-permute-start.3 = (f32[2,16,1]{2,1,0:T(8,128)S(1)}, f32[2,16,1]{2,1,0:T(8,128)S(1)}, u32[]{:S(2)}, u32[]{:S(2)}) collective-permute-start(f32[2,16,1]{2,1,0:T(8,128)S(1)} %get-tuple-element.89), channel_id=1, source_target_pairs={{1,0},{2,1},{3,2},{4,3},{5,4},{6,5},{7,6},{8,7},{9,8},{10,9},{11,1... | collective-permute-start | bytes 392 | tf_op jit(solution)/shard_map/ppermute | solution.py:22
  32.4 1.9 collective-permute-start.2
  34.5 5.1 %collective-permute-done.2 = f32[2,16,1]{2,1,0:T(8,128)S(1)} collective-permute-done((f32[2,16,1]{2,1,0:T(8,128)S(1)}, f32[2,16,1]{2,1,0:T(8,128)S(1)}, u32[]{:S(2)}, u32[]{:S(2)}) %collective-permute-start.2) | collective-permute-done | bytes 160 | tf_op jit(solution)/shard_map/ppermute | solution.py:19
  39.6 2.4 %concatenate.39 = f32[2,16,16386]{2,1,0:T(8,128)} concatenate(f32[2,16,1]{2,1,0:T(8,128)S(1)} %collective-permute-done.2, f32[2,16,16384]{2,1,0:T(8,128)S(1)} %pad_maximum_fusion.1, f32[2,16,1]{2,1,0:T(8,128)S(1)} %collective-permute-done.3), dimensions={2} | concatenate | bytes 4194816 | tf_op jit(solution)/shard_map/concatenate | solution.py:23
  42.0 1.7 slice_bitcast_fusion.1
  43.6 3.3 %fusion.19 = (f32[16,16385]{1,0:T(8,128)S(1)}, f32[16,16385]{1,0:T(8,128)S(1)}, f32[16,16385]{1,0:T(8,128)}, f32[16,16385]{1,0:T(8,128)}) fusion(f32[16,16386]{1,0:T(8,128)S(1)} %get-tuple-element.84, pred[16385]{0:T(1024)(128)(4,1)S(1)} %fusion.58, f32[16,16386]{1,0:T(8,128)S(1)} %get-tuple-element.83), kind=kLoop, calls=%fused_computation.50 | loop fusion | flops 10748560 | bytes 8405505 | tf_op jit(solution)/shard_map/div | solution.py:63
  47.5 4.6 %copy.181 = f32[16,16384]{0,1:T(8,128)} copy(f32[16,16384]{1,0:T(8,128)S(1)} %fusion.35) | data formatting | bytes 2097152 | tf_op jit(solution)/shard_map/add | solution.py:76
  52.8 1.9 collective-permute-start.4
  54.7 5.8 %collective-permute-start.5 = (f32[18,512]{1,0:T(8,128)}, f32[18,512]{1,0:T(8,128)}, u32[]{:S(2)}, u32[]{:S(2)}) collective-permute-start(f32[18,512]{1,0:T(8,128)} %get-tuple-element.96), channel_id=1, source_target_pairs={{1,0},{2,1},{3,2},{4,3},{5,4},{6,5},{7,6},{8,7},{9,8},{10,9},{11,1... | collective-permute-start | bytes 110600 | tf_op jit(solution)/shard_map/ppermute | solution.py:22
  60.5 5.0 %gather_fusion = f32[512,16]{1,0:T(8,128)} fusion(f32[16,16384]{0,1:T(8,128)} %copy.181, s32[1024]{0:T(1024)S(1)} %pad_clamp_fusion), kind=kCustom, calls=%fused_computation | custom fusion | bytes 67584 | tf_op jit(solution)/shard_map/gather | solution.py:144
  65.5 1.0 copy.182
  66.5 12.5 %all-gather = f32[64,512]{1,0:T(8,128)S(1)} all-gather(f32[16,512]{1,0:T(8,128)S(1)} %copy.182), channel_id=2, replica_groups=mesh['mem'=4,'cell'=64] {'mem'}, dimensions={0}, use_global_device_ids=true | all-gather | bytes 163840 | tf_op jit(solution)/shard_map/all_gather | solution.py:145
  82.2 5.4 %all-to-all-start.2 = ((f32[64,1,2]{2,1,0:T(1,128)}), f32[64,1,2]{2,1,0:T(1,128)S(1)}, u32[]{:S(2)}, u32[]{:S(2)}) async-start(f32[64,1,2]{2,1,0:T(1,128)} %broadcast_in_dim.63), calls=%async_computation.2 | async-start | bytes 65536 | tf_op jit(solution)/shard_map/all_to_all | solution.py:29
  87.7 2.4 %fusion.31 = f32[16,16384]{1,0:T(8,128)S(1)} fusion(f32[16,16385]{1,0:T(8,128)S(1)} %get-tuple-element.79, f32[16,16385]{1,0:T(8,128)} %get-tuple-element.98, f32[16,16385]{1,0:T(8,128)} %get-tuple-element.97, f32[16,16386]{1,0:T(8,128)S(1)} %get-tuple-element.84, pred[16384]{0:T(1024)(128)(4,1)S(1)} %get-tuple-element.106, ...), kind=kLoop, calls=%fused_computation.80 | loop fusion | flops 2359296 | bytes 6324224 | tf_op jit(solution)/shard_map/sub | solution.py:77
  90.1 1.0 copy.225
  91.2 5.1 %all-to-all-done.2 = f32[64,1,2]{2,1,0:T(1,128)S(1)} async-done(((f32[64,1,2]{2,1,0:T(1,128)}), f32[64,1,2]{2,1,0:T(1,128)S(1)}, u32[]{:S(2)}, u32[]{:S(2)}) %all-to-all-start.2) | async-done | bytes 544 | tf_op jit(solution)/shard_map/all_to_all | solution.py:29
  96.9 3.8 %all-to-all-start.1 = ((f32[16,4,4096]{2,0,1:T(8,128)}), f32[16,4,4096]{2,0,1:T(8,128)S(1)}, u32[]{:S(2)}, u32[]{:S(2)}) async-start(f32[16,4,4096]{2,0,1:T(8,128)} %bitcast.126), calls=%async_computation.1 | async-start | bytes 2097152 | tf_op jit(solution)/shard_map/all_to_all | solution.py:162
  100.7 2.7 %pad_maximum_fusion.6 = (f32[18,16384]{1,0:T(8,128)}, f32[18,16384]{1,0:T(8,128)}) fusion(f32[18,512]{1,0:T(8,128)} %collective-permute-done.4, f32[1,16384]{1,0:T(1,128)S(1)} %bitcast.138, f32[1,16384]{1,0:T(1,128)S(1)} %bitcast.142, f32[16,16384]{1,0:T(8,128)S(1)} %fusion.35, f32[18,512]{1,0:T(8,128)} %collective-permute-done.5), kind=kLoop, calls=%fused_computation.31 | loop fusion | flops 1769472 | bytes 3612672 | tf_op jit(solution)/shard_map/concatenate | solution.py:23
  103.3 2.1 reshape.165
  105.5 3.0 %reshape.166 = f32[18,4,4096]{2,1,0:T(4,128)} reshape(f32[18,16384]{1,0:T(8,128)} %get-tuple-element.94) | data formatting | bytes 2359296 | tf_op jit(solution)/shard_map/reshape | solution.py:155
  108.6 0.9 slice.261
  110.2 1.2 slice.262
  111.4 4.4 %all-to-all-done.1 = f32[16,4,4096]{2,0,1:T(8,128)S(1)} async-done(((f32[16,4,4096]{2,0,1:T(8,128)}), f32[16,4,4096]{2,0,1:T(8,128)S(1)}, u32[]{:S(2)}, u32[]{:S(2)}) %all-to-all-start.1) | async-done | bytes 1048608 | tf_op jit(solution)/shard_map/all_to_all | solution.py:162
  115.8 3.5 %all-to-all-start = ((f32[16,4,5120]{2,0,1:T(8,128)}), f32[16,4,5120]{2,0,1:T(8,128)S(1)}, u32[]{:S(2)}, u32[]{:S(2)}) async-start(f32[16,4,5120]{2,0,1:T(8,128)} %slice.262), calls=%async_computation | async-start | bytes 2621440 | tf_op jit(solution)/shard_map/all_to_all | solution.py:161
  124.2 1.6 copy.211
  125.7 10.6 %all-to-all-done = f32[16,4,5120]{2,0,1:T(8,128)S(1)} async-done(((f32[16,4,5120]{2,0,1:T(8,128)}), f32[16,4,5120]{2,0,1:T(8,128)S(1)}, u32[]{:S(2)}, u32[]{:S(2)}) %all-to-all-start) | async-done | bytes 1310752 | tf_op jit(solution)/shard_map/all_to_all | solution.py:161
  139.4 1.7 squeeze.49
  141.0 1.9 subtract_multiply_fusion
  142.9 2.8 %fusion.43 = f32[10,64,64]{2,1,0:T(8,128)S(1)} fusion(f32[64,10,512]{2,1,0:T(8,128)S(1)} %subtract_multiply_fusion), kind=kOutput, calls=%fused_computation.98 | convolution fusion | flops 251658240 | bytes 1474560 | tf_op jit(solution)/shard_map/ibr,jbr->bij/dot_general | solution.py:173
  145.7 2.0 fusion.41
  148.1 19.9 %while.14 = (s32[]{:T(128)}, f32[8,64,64]{1,2,0:T(8,128)S(1)}, f32[8,64,64]{2,1,0:T(8,128)S(1)}, s32[]{:T(128)}) while((s32[]{:T(128)}, f32[8,64,64]{1,2,0:T(8,128)S(1)}, f32[8,64,64]{2,1,0:T(8,128)S(1)}, s32[]{:T(128)}) %tuple.59), condition=%wide.region_10.11_spmd.clone, body=%wide.region_9.10_spmd.clone.sunk | while | flops 75571200 | bytes 1736757 | solution.py:98
  168.9 2.1 %bitcast_add_fusion = f32[2,64,8,512]{3,1,0,2:T(8,128)S(1)} fusion(f32[2,64,8,512]{3,1,0,2:T(8,128)S(1)} %copy_dynamic-update-slice_fusion, f32[2,8,512]{2,0,1:T(2,128)S(1)} %broadcast_multiply_fusion, f32[8,64,64]{2,1,0:T(8,128)S(1)} %get-tuple-element.36, f32[8,64]{1,0:T(8,128)S(1)} %broadcast_multiply_fusion.2, f32[8]{0:T(128)S(1)} %get-tuple-element.109, ...), kind=kOutput, calls=%fused_computation.19 | convolution fusion | flops 403800064 | bytes 4360228 | tf_op jit(solution)/shard_map/fipr,pij->fjpr/dot_general | solution.py:184
  171.1 1.2 copy.203
  172.3 2.8 %reshape.201 = f32[2,64,4096]{2,0,1:T(2,128)} reshape(f32[2,64,8,512]{3,2,0,1:T(8,128)S(1)} %copy.203) | data formatting | bytes 4194304 | tf_op jit(solution)/shard_map/reshape | solution.py:188
  175.1 28.2 %all_to_all.51 = f32[2,64,4096]{2,0,1:T(2,128)S(1)} all-to-all(f32[2,64,4096]{2,0,1:T(2,128)} %reshape.201), channel_id=1, replica_groups=mesh['mem'=4,'cell'=64] {'mem'}, dimensions={1} | all-to-all | bytes 4194304 | tf_op jit(solution)/shard_map/all_to_all | solution.py:187
  203.3 1.2 copy.190
  205.4 1.6 copy.213
  207.7 1.6 copy.212
  (157 shorter events, 34.7 us)
Async XLA Ops:
  1.5 10.1 %copy-start.1 = (f32[16,16384]{1,0:T(8,128)S(1)}, f32[16,16384]{1,0:T(8,128)}, u32[]{:S(2)}) copy-start(f32[16,16384]{1,0:T(8,128)} %param.12) | copy-start | bytes 3145732
  1.5 10.1 %copy-start.2 = (f32[16,16384]{1,0:T(8,128)S(1)}, f32[16,16384]{1,0:T(8,128)}, u32[]{:S(2)}) copy-start(f32[16,16384]{1,0:T(8,128)} %param.13) | copy-start | bytes 3145732
  2.5 17.3 %collective-permute-start.1 = (f32[2,16,1]{2,1,0:T(8,128)S(1)}, f32[2,16,1]{2,1,0:T(8,128)S(1)}, u32[]{:S(2)}, u32[]{:S(2)}) collective-permute-start(f32[2,16,1]{2,1,0:T(8,128)S(1)} %get-tuple-element.91), channel_id=1, source_target_pairs={{1,0},{2,1},{3,2},{4,3},{5,4},{6,5},{7,6},{8,7},{9,8},{10,9},{11,1... | collective-permute-start | bytes 392 | tf_op jit(solution)/shard_map/ppermute | solution.py:22
  9.6 10.1 %collective-permute-start = (f32[2,16,1]{2,1,0:T(8,128)S(1)}, f32[2,16,1]{2,1,0:T(8,128)S(1)}, u32[]{:S(2)}, u32[]{:S(2)}) collective-permute-start(f32[2,16,1]{2,1,0:T(8,128)S(1)} %get-tuple-element.92), channel_id=1, source_target_pairs={{0,1},{1,2},{2,3},{3,4},{4,5},{5,6},{6,7},{7,8},{8,9},{9,10},{10,1... | collective-permute-start | bytes 392 | tf_op jit(solution)/shard_map/ppermute | solution.py:19
  11.6 1.5 copy-start.11
  11.6 1.5 copy-start.12
  11.6 2.8 %copy-start.6 = (s32[2,16384]{1,0:T(2,128)S(1)}, s32[2,16384]{1,0:T(2,128)}, u32[]{:S(2)}) copy-start(s32[2,16384]{1,0:T(2,128)} %param.15) | copy-start | bytes 393220
  11.6 5.4 %copy-start.9 = (f32[16384]{0:T(1024)S(1)}, f32[16384]{0:T(1024)}, u32[]{:S(2)}) copy-start(f32[16384]{0:T(1024)} %param.16) | copy-start | bytes 196612
  26.7 7.8 %collective-permute-start.3 = (f32[2,16,1]{2,1,0:T(8,128)S(1)}, f32[2,16,1]{2,1,0:T(8,128)S(1)}, u32[]{:S(2)}, u32[]{:S(2)}) collective-permute-start(f32[2,16,1]{2,1,0:T(8,128)S(1)} %get-tuple-element.89), channel_id=1, source_target_pairs={{1,0},{2,1},{3,2},{4,3},{5,4},{6,5},{7,6},{8,7},{9,8},{10,9},{11,1... | collective-permute-start | bytes 392 | tf_op jit(solution)/shard_map/ppermute | solution.py:22
  32.4 7.2 %collective-permute-start.2 = (f32[2,16,1]{2,1,0:T(8,128)S(1)}, f32[2,16,1]{2,1,0:T(8,128)S(1)}, u32[]{:S(2)}, u32[]{:S(2)}) collective-permute-start(f32[2,16,1]{2,1,0:T(8,128)S(1)} %get-tuple-element.90), channel_id=1, source_target_pairs={{0,1},{1,2},{2,3},{3,4},{4,5},{5,6},{6,7},{7,8},{8,9},{9,10},{10,1... | collective-permute-start | bytes 392 | tf_op jit(solution)/shard_map/ppermute | solution.py:19
  52.1 26.9 %copy-start.10 = (f32[1,512]{1,0:T(1,128)S(1)}, f32[1,512]{1,0:T(1,128)}, u32[]{:S(2)}) copy-start(f32[1,512]{1,0:T(1,128)} %param.18) | copy-start | bytes 6148
  52.8 47.9 %collective-permute-start.4 = (f32[18,512]{1,0:T(8,128)}, f32[18,512]{1,0:T(8,128)}, u32[]{:S(2)}, u32[]{:S(2)}) collective-permute-start(f32[18,512]{1,0:T(8,128)} %get-tuple-element.95), channel_id=1, source_target_pairs={{0,1},{1,2},{2,3},{3,4},{4,5},{5,6},{6,7},{7,8},{8,9},{9,10},{10,1... | collective-permute-start | bytes 110600 | tf_op jit(solution)/shard_map/ppermute | solution.py:19
  54.7 46.0 %collective-permute-start.5 = (f32[18,512]{1,0:T(8,128)}, f32[18,512]{1,0:T(8,128)}, u32[]{:S(2)}, u32[]{:S(2)}) collective-permute-start(f32[18,512]{1,0:T(8,128)} %get-tuple-element.96), channel_id=1, source_target_pairs={{1,0},{2,1},{3,2},{4,3},{5,4},{6,5},{7,6},{8,7},{9,8},{10,9},{11,1... | collective-permute-start | bytes 110600 | tf_op jit(solution)/shard_map/ppermute | solution.py:22
  82.2 14.1 %all-to-all-start.2 = ((f32[64,1,2]{2,1,0:T(1,128)}), f32[64,1,2]{2,1,0:T(1,128)S(1)}, u32[]{:S(2)}, u32[]{:S(2)}) async-start(f32[64,1,2]{2,1,0:T(1,128)} %broadcast_in_dim.63), calls=%async_computation.2 | async-start | bytes 65536 | tf_op jit(solution)/shard_map/all_to_all | solution.py:29
  96.3 0.6 copy-start.7
  96.9 18.9 %all-to-all-start.1 = ((f32[16,4,4096]{2,0,1:T(8,128)}), f32[16,4,4096]{2,0,1:T(8,128)S(1)}, u32[]{:S(2)}, u32[]{:S(2)}) async-start(f32[16,4,4096]{2,0,1:T(8,128)} %bitcast.126), calls=%async_computation.1 | async-start | bytes 2097152 | tf_op jit(solution)/shard_map/all_to_all | solution.py:162
  105.5 4.1 %copy-start.3 = (f32[18,4,512]{2,0,1:T(8,128)}, f32[18,4,512]{2,0,1:T(8,128)S(1)}, u32[]{:S(2)}) copy-start(f32[18,4,512]{2,0,1:T(8,128)S(1)} %copy.176) | copy-start | bytes 442372
  109.5 0.7 copy-start.4
  115.8 20.6 %all-to-all-start = ((f32[16,4,5120]{2,0,1:T(8,128)}), f32[16,4,5120]{2,0,1:T(8,128)S(1)}, u32[]{:S(2)}, u32[]{:S(2)}) async-start(f32[16,4,5120]{2,0,1:T(8,128)} %slice.262), calls=%async_computation | async-start | bytes 2621440 | tf_op jit(solution)/shard_map/all_to_all | solution.py:161
  137.2 1.2 copy-start
  139.3 1.7 copy-start.8
  145.7 2.0 copy-start.5
where the time goes:
time: 210 us; the launch traced here: 209 us
  local copies, waits for them, and re-layouts  52.3 us (25%)
  blocking collectives  40.7 us (19%)
  starting transfers between devices  37.1 us (18%)
  matrix products  26.1 us (12%)
  waiting for transfers between devices  25.2 us (12%)
  other arithmetic  23.1 us (11%)
  between operations  3.68 us (2%)
    all_to_all x1, blocking collectives, shards(): lax.all_to_all(analysed.reshape(2, members, quart_cells), 'mem', split_ax...  28.2 us
    dot_general x37, matrix products, batch_product(): jnp.einsum('uij,ujk->uik', first, second, precision=lax.Precision.HIGHEST)  18.8 us
    ppermute x3, starting transfers between devices, padded_2(): lax.ppermute(lax.slice_in_dim(block, 0, width, axis=dim), axis, backward)  18.7 us
    all_gather x1, blocking collectives, shards(): seen_all = lax.all_gather(seen_local, 'mem', axis=0, tiled=True)  12.5 us
    all_to_all x1, waiting for transfers between devices, shards(): lax.all_to_all(windows[:member_rows], 'mem', split_axis=1, concat_axis=0,...  10.6 us
    unnamed x33, local copies, waits for them, and re-layouts  8.67 us
    gather x2, local copies, waits for them, and re-layouts, shards(): seen_local = depth_now[:, offsets]  6.07 us
    ppermute x3, starting transfers between devices, padded_2(): lax.ppermute(lax.slice_in_dim(block, block.shape[dim] - width, None, axis...  5.75 us
  transfers between devices with their start and end apart: 9, of which 4 were waited for; matrix products, arithmetic and copies ran while one was open for 17% of the time, Pallas kernels for 0%

commit v1 on v0

v1 whole, which is shorter than its diff:
```python
import functools
import jax
import jax.numpy as jnp
from jax import lax
from jax.experimental import pallas as pl
from jax.experimental.pallas import tpu as pltpu
from jax.sharding import PartitionSpec as P

PER = 512
NS_ITERS = 12
gravity = 9.81
step_dt = 0.06
LANE = 128
F32 = jnp.float32
BF16 = jnp.bfloat16


def mm(a, b, dims=((1,), (0,))):
    return lax.dot_general(a, b, (dims, ((), ())), precision=lax.Precision.HIGHEST, preferred_element_type=F32)


def window_step(h, q, gate, inflow):
    back = h.shape[1] - 1
    gh = gravity * h
    u = q * (1.0 / h)
    c = gh * lax.rsqrt(gh)
    slow = u - c
    fast = u + c
    pressure = (0.5 * gh) * h
    moment = q * u + pressure
    hl = pltpu.roll(h, 1, 1)
    ql = pltpu.roll(q, 1, 1)
    a = jnp.minimum(jnp.minimum(pltpu.roll(slow, 1, 1), slow), 0.0)
    b = jnp.maximum(jnp.maximum(pltpu.roll(fast, 1, 1), fast), 0.0)
    ml = pltpu.roll(moment, 1, 1)
    inv = 1.0 / (b - a)
    ab = a * b
    mass = (b * ql - a * q + ab * (h - hl)) * inv
    mom = (b * ml - a * moment + ab * (q - ql)) * inv
    opened = jnp.broadcast_to(gate, h.shape) > 0.5
    opened_next = jnp.broadcast_to(pltpu.roll(gate, back, 1), h.shape) > 0.5
    mass = jnp.where(opened, mass, 0.0)
    right_side = jnp.where(opened, mom, pressure)
    left_side = jnp.where(opened_next, pltpu.roll(mom, back, 1), pressure)
    h_new = h - step_dt * (pltpu.roll(mass, back, 1) - mass) + inflow
    q_new = q - step_dt * (left_side - right_side)
    return h_new, q_new


def forecast_kernel(
    depth, flow, gate, pump, rate, low, high, offsets, *refs
):
    *fields, seen, h0, q0, h1, q1, rows, table = refs
    members, cells = depth.shape
    quarters = len(fields)
    quart = cells // quarters
    pad = 2 * LANE
    total = cells + 2 * pad
    end = pad + cells
    h0[:, pad:end] = depth[...]
    q0[:, pad:end] = flow[...]
    h0[:, pad - LANE : pad] = low[0:members, :]
    q0[:, pad - LANE : pad] = low[members : 2 * members, :]
    h0[:, end : end + LANE] = high[0:members, :]
    q0[:, end : end + LANE] = high[members : 2 * members, :]
    for r in range(2):
        h0[:, r * (total - LANE) : r * (total - LANE) + LANE] = jnp.ones((members, LANE), F32)
        q0[:, r * (total - LANE) : r * (total - LANE) + LANE] = jnp.zeros((members, LANE), F32)
        rows[:, r * (total - LANE) : r * (total - LANE) + LANE] = jnp.zeros((8, LANE), F32)
    rows[0:1, pad:end] = gate[...].astype(F32)
    rows[1:2, pad:end] = step_dt * (rate[...] * pump[0:1, :].astype(F32))
    rows[2:3, pad:end] = step_dt * (rate[...] * pump[1:2, :].astype(F32))
    rows[0:1, pad - LANE : pad] = low[2 * members : 2 * members + 1, :]
    rows[1:2, pad - LANE : pad] = low[2 * members + 1 : 2 * members + 2, :]
    rows[0:1, end : end + LANE] = high[2 * members : 2 * members + 1, :]
    rows[1:2, end : end + LANE] = high[2 * members + 1 : 2 * members + 2, :]
    first = lax.axis_index("cell") == 0
    lane = lax.broadcasted_iota(jnp.int32, (1, LANE), 1)
    shut = jnp.where(first, 1, 0) * jnp.where(lane == 0, 1, 0)
    rows[0:1, pad : pad + LANE] = jnp.where(shut > 0, 0.0, rows[0:1, pad : pad + LANE])

    w1 = 26 * LANE

    def first_step(i, _):
        at = pl.ds(pl.multiple_of(i * w1, LANE), w1 + 2 * LANE)
        h, q = window_step(h0[:, at], q0[:, at], rows[0:1, at], rows[1:2, at])
        put = pl.ds(pl.multiple_of(i * w1 + LANE, LANE), w1)
        h1[:, put] = h[:, LANE : LANE + w1]
        q1[:, put] = q[:, LANE : LANE + w1]
        return 0

    lax.fori_loop(0, (cells + 2 * LANE) // w1, first_step, 0)
    w2 = 16 * LANE
    for k in range(quarters):
        first_tile = lax.rem(lax.axis_index("mem") + k, quarters) * (quart // LANE)

        def second_step(i, _):
            tile = first_tile + i * (w2 // LANE)
            at = pl.ds(pl.multiple_of(pad - LANE + tile * LANE, LANE), w2 + 2 * LANE)
            h, q = window_step(h1[:, at], q1[:, at], rows[0:1, at], rows[2:3, at])
            h = h[:, LANE : LANE + w2]
            put = pl.ds(pl.multiple_of(i * w2, LANE), w2)
            fields[k][0, :, put] = h
            fields[k][1, :, put] = q[:, LANE : LANE + w2]
            for t in range(w2 // LANE):
                table[tile + t] = h[:, t * LANE : (t + 1) * LANE]
            return 0

        lax.fori_loop(0, quart // w2, second_step, 0)
    lanes = lax.broadcasted_iota(jnp.int32, (members, LANE), 1)

    def pick(g, _):
        acc = jnp.zeros((members, LANE), F32)
        for k in range(LANE):
            spot = offsets[g * LANE + k]
            row = table[lax.shift_right_logical(spot, 7)]
            turn = jnp.bitwise_and(k - spot, LANE - 1)
            acc = jnp.where(lanes == k, pltpu.roll(row, turn, 1), acc)
        for m in range(quarters):
            seen[m, :, pl.ds(pl.multiple_of(g * LANE, LANE), LANE)] = acc
        return 0

    lax.fori_loop(0, seen.shape[2] // LANE, pick, 0)


def message_kernel(*refs):
    for end in range(2):
        depth, flow, gate, pump, rate = refs[5 * end : 5 * end + 5]
        out = refs[10 + end]
        n = depth.shape[0]
        out[0:n] = depth[...]
        out[n : 2 * n] = flow[...]
        out[2 * n : 2 * n + 1] = gate[...].astype(F32)
        out[2 * n + 1 : 2 * n + 2] = step_dt * (rate[...] * pump[0:1].astype(F32))
        out[2 * n + 2 :] = jnp.zeros((6, LANE), F32)


def scaled_obs(seen_ref, value, error):
    groups = seen_ref.shape[0]
    mem = lax.axis_index("mem")
    seen = jnp.concatenate([seen_ref[lax.rem(mem + groups - k, groups)] for k in range(groups)], axis=0)
    mean = jnp.mean(seen, axis=0, keepdims=True)
    precision = 1.0 / error
    return (seen - mean) * precision, (value - mean) * precision


def totals_kernel(seen, value, error, offsets, *refs, last):
    totals, edge = refs[3:5]
    scaled, innov = scaled_obs(seen, value[...], error[...])
    members = scaled.shape[0]
    misfit = jnp.sum(innov * innov, axis=(0, 1), keepdims=True)
    spread = jnp.sum(scaled * scaled, axis=(0, 1), keepdims=True) / (members - 1)
    lane = lax.broadcasted_iota(jnp.int32, totals.shape, 1)
    totals[...] = jnp.where(lane == 0, misfit, jnp.where(lane == 1, spread, 0.0))
    upper = lax.axis_index("mem") == lax.axis_size("mem") - 1
    here = jnp.where(upper, 0, last)
    masked = jnp.where(offsets[...] // PER == here, scaled, 0.0)
    extended = jnp.concatenate([scaled, jnp.broadcast_to(innov, (8, innov.shape[1]))], axis=0)
    edge[...] = mm(extended, masked, ((1,), (1,)))


def split(x):
    top = x.astype(BF16)
    rest = x - top.astype(F32)
    middle = rest.astype(BF16)
    return top, middle, (rest - middle.astype(F32)).astype(BF16)


def dot(a, b):
    return lax.dot_general(a, b, (((1,), (0,)), ((), ())), preferred_element_type=F32)


def transform_kernel(seen, value, error, offsets, totals, edge, mixing, weights, *, total_obs):
    scaled, innov = scaled_obs(seen, value[...], error[...])
    members = scaled.shape[0]
    pack = 4
    groups = mixing.shape[0]
    wide = pack * members
    weights[...] = jnp.zeros(weights.shape, BF16)
    extended = jnp.concatenate([scaled, jnp.broadcast_to(innov, (8, innov.shape[1]))], axis=0)
    mem = lax.axis_index("mem")
    polder = offsets[...] // PER - mem * (groups * pack)
    sums = jnp.sum(totals[...], axis=0, keepdims=True)
    lane = lax.broadcasted_iota(jnp.int32, sums.shape, 1)
    misfit = jnp.sum(jnp.where(lane == 0, sums, 0.0), axis=(0, 1), keepdims=True)
    spread = jnp.sum(jnp.where(lane == 1, sums, 0.0), axis=(0, 1), keepdims=True)
    rho2 = misfit / (spread + total_obs)
    rho = jnp.sqrt(rho2)
    r64 = lax.broadcasted_iota(jnp.int32, (members, wide), 0)
    c64 = lax.broadcasted_iota(jnp.int32, (members, wide), 1)
    eye = jnp.where(r64 == c64 % members, 1.0, 0.0)
    half = lax.broadcasted_iota(jnp.int32, (members, LANE), 1) // members
    keep = [jnp.where(half == k, 1.0, 0.0).astype(BF16) for k in range(2)]

    def load_weights(g, parts):
        for p, part in enumerate(parts):
            for k in range(pack):
                cols = slice((k // 2) * LANE, (k // 2 + 1) * LANE)
                weights[g, p, k * members : (k + 1) * members, cols] = part[:, cols] * keep[k % 2]

    def product(g, pieces):
        n = [p[0].shape[0] for p in pieces]
        total = [None] * len(pieces)
        for w, depth in ((2, 1), (1, 2), (0, 3)):
            stack = jnp.concatenate([p[d] for p in pieces for d in range(depth)], axis=0)
            y = dot(stack, weights[g, w])
            at = 0
            for i in range(len(pieces)):
                slabs = [y[at + d * n[i] : at + (d + 1) * n[i]] for d in range(depth)]
                at += depth * n[i]
                piece = slabs[-1]
                for z in reversed(slabs[:-1]):
                    piece = piece + z
                total[i] = piece if total[i] is None else total[i] + piece
        return total

    low_edge = jnp.where(mem == 0, 1.0, 0.0)
    high_edge = jnp.where(mem == lax.axis_size("mem") - 1, 1.0, 0.0)
    wide_edge = jnp.concatenate([edge[...]] * pack, axis=1)
    e_col = lax.broadcasted_iota(jnp.int32, wide_edge.shape, 1) // members
    starts = []
    for g in range(groups):
        picked = jnp.concatenate(
            [jnp.where(jnp.abs(polder - (g * pack + k)) <= 1, scaled, 0.0) for k in range(pack)], axis=0
        )
        gram = mm(extended, picked, ((1,), (1,)))
        if g == 0:
            gram = gram + jnp.where(e_col == 0, wide_edge * low_edge, 0.0)
        if g == groups - 1:
            gram = gram + jnp.where(e_col == pack - 1, wide_edge * high_edge, 0.0)
        system = eye + rho2 / (members - 1) * gram[:members]
        squares = jnp.sum(system * system, axis=0, keepdims=True)
        column = lax.broadcasted_iota(jnp.int32, squares.shape, 1) // members
        norm2 = jnp.zeros_like(squares)
        for k in range(pack):
            here = jnp.where(column == k, squares, 0.0)
            norm2 = jnp.where(column == k, jnp.sum(here, axis=1, keepdims=True), norm2)
        norm = jnp.sqrt(norm2)
        starts.append((system / norm, gram[members : members + 8], norm))

    def iterate(turn, carry):
        out = []
        for g in range(groups):
            energy, inverse = carry[g]
            parts = split(energy)
            load_weights(g, parts)
            square, step = product(g, [parts, split(inverse)])
            factor = 2.25 * eye - 1.5 * energy + 0.25 * square
            out.append((product(g, [split(factor)])[0], 1.5 * inverse - 0.5 * step))
        return tuple(out)

    carry = lax.fori_loop(0, NS_ITERS, iterate, tuple((s[0], eye) for s in starts))
    for g in range(groups):
        _, cross, norm = starts[g]
        inverse = carry[g][1]
        load_weights(g, split(inverse))
        solved = product(g, [split(product(g, [split(cross)])[0])])[0]
        weight = (rho / (members - 1)) * solved[0:1] / norm
        mixing[g] = rho * (inverse / jnp.sqrt(norm) + weight)


def apply_kernel(*refs):
    quarters = len(refs) // 2
    fields, mixing, out = refs[:quarters], refs[quarters], refs[quarters + 1 :]
    _, rows, width = fields[0].shape
    members = quarters * rows
    for u in range(width // PER):
        mix = mixing[u // 4, :, (u % 4) * members : (u % 4 + 1) * members]
        mix_hi = mix.astype(BF16)
        mix_lo = (mix - mix_hi.astype(F32)).astype(BF16)
        left = jnp.concatenate([mix_hi, mix_hi, mix_lo, mix_lo], axis=1)
        cols = slice(u * PER, (u + 1) * PER)
        for f in range(2):
            x = jnp.concatenate([part[f, :, cols] for part in fields], axis=0)
            mean = jnp.mean(x, axis=0, keepdims=True)
            d = x - mean
            d_hi = d.astype(BF16)
            d_lo = (d - d_hi.astype(F32)).astype(BF16)
            y = dot(left, jnp.concatenate([d_hi, d_lo, d_hi, d_lo], axis=0)) + mean
            for k in range(quarters):
                out[k][f, :, cols] = y[k * rows : (k + 1) * rows]


def assemble_kernel(*refs):
    *parts, depth, flow, sems = refs
    quarters = len(parts)
    quart = parts[0].shape[2]
    copies = []
    for k in range(quarters):
        at = lax.rem(lax.axis_index("mem") + k, quarters) * quart
        for f, target in enumerate((depth, flow)):
            to = target.at[:, pl.ds(pl.multiple_of(at, LANE), quart)]
            copies.append(pltpu.make_async_copy(parts[k].at[f], to, sems.at[k, f]))
    for c in copies:
        c.start()
    for c in copies:
        c.wait()


VM = pl.BlockSpec(memory_space=pltpu.VMEM)
SM = pl.BlockSpec(memory_space=pltpu.SMEM)
ANY = pl.BlockSpec(memory_space=pl.ANY)


def vmem(mib):
    return pltpu.CompilerParams(vmem_limit_bytes=mib << 20)


def shards(depth, discharge, gate, pump, pump_rate, obs_index, obs_value, obs_error):
    rows, cells = depth.shape
    quarters = lax.axis_size("mem")
    slabs = lax.axis_size("cell")
    members = rows * quarters
    quart = cells // quarters
    obs = obs_index.shape[1]
    gate_row = gate.reshape(1, cells)
    rate_row = pump_rate.reshape(1, cells)

    tiles = cells // LANE

    def edge_specs(tile):
        return [pl.BlockSpec((n, LANE), lambda i: (0, tile)) for n in (rows, rows, 1, 2, 1)]

    whole = pl.BlockSpec((2 * rows + 8, LANE), lambda i: (0, 0))
    ends = pl.pallas_call(
        message_kernel,
        grid=(1,),
        out_shape=(jax.ShapeDtypeStruct((2 * rows + 8, LANE), F32),) * 2,
        in_specs=edge_specs(tiles - 1) + edge_specs(0),
        out_specs=(whole, whole),
        name="message",
    )(*((depth, discharge, gate_row, pump, rate_row) * 2))
    up = [(i, i + 1) for i in range(slabs - 1)]
    down = [(i + 1, i) for i in range(slabs - 1)]
    low = lax.ppermute(ends[0], "cell", up)
    high = lax.ppermute(ends[1], "cell", down)
    total = cells + 4 * LANE
    block = jax.ShapeDtypeStruct((2, rows, quart), F32)
    own, *sent, seen = pl.pallas_call(
        forecast_kernel,
        out_shape=(block,) * quarters + (jax.ShapeDtypeStruct((quarters, rows, obs), F32),),
        in_specs=[VM] * 7 + [SM],
        out_specs=(VM,) * (quarters + 1),
        scratch_shapes=[pltpu.VMEM((rows, total), F32)] * 4
        + [pltpu.VMEM((8, total), F32), pltpu.VMEM((cells // LANE, rows, LANE), F32)],
        compiler_params=vmem(24),
        name="forecast",
    )(depth, discharge, gate_row, pump, rate_row, low, high, obs_index.reshape(obs))
    seen_all = lax.all_to_all(seen, "mem", split_axis=0, concat_axis=0, tiled=True)
    totals, edge, *sent = pl.pallas_call(
        functools.partial(totals_kernel, last=cells // PER - 1),
        out_shape=(
            jax.ShapeDtypeStruct((slabs, LANE), F32),
            jax.ShapeDtypeStruct((members + 8, members), F32),
        )
        + (block,) * 3,
        in_specs=[VM, VM, VM, VM, ANY, ANY, ANY],
        out_specs=(VM, VM, ANY, ANY, ANY),
        input_output_aliases={4: 2, 5: 3, 6: 4},
        compiler_params=vmem(8),
        name="totals",
    )(seen_all, obs_value, obs_error, obs_index, *sent)

    def turned(x, by):
        return lax.ppermute(x, "mem", [(i, (i + by) % quarters) for i in range(quarters)])

    moved = [own] + [turned(x, k) for k, x in enumerate(sent, 1)]
    top = quarters - 1
    pairs = [(i, i + 1) for i in range(slabs - 1)]
    pairs += [(top * slabs + i + 1, top * slabs + i) for i in range(slabs - 1)]
    edge = lax.ppermute(edge, ("mem", "cell"), pairs)
    everyone = lax.all_to_all(totals, "cell", split_axis=0, concat_axis=0, tiled=True)
    groups = quart // PER // 4
    mixing = pl.pallas_call(
        functools.partial(transform_kernel, total_obs=float(obs * slabs)),
        out_shape=jax.ShapeDtypeStruct((groups, members, 4 * members), F32),
        in_specs=[VM] * 6,
        out_specs=VM,
        scratch_shapes=[pltpu.VMEM((groups, 3, 4 * members, 4 * members), BF16)],
        compiler_params=vmem(12),
        name="transform",
    )(seen_all, obs_value, obs_error, obs_index, everyone, edge)
    kept, *given = pl.pallas_call(
        apply_kernel,
        out_shape=(block,) * quarters,
        in_specs=[VM] * (quarters + 1),
        out_specs=(VM,) * quarters,
        compiler_params=vmem(14),
        name="apply",
    )(*moved, mixing)
    parts = [kept] + [turned(x, -k) for k, x in enumerate(given, 1)]
    out = jax.ShapeDtypeStruct((rows, cells), F32)
    return pl.pallas_call(
        assemble_kernel,
        out_shape=(out, out),
        in_specs=[VM] * quarters,
        out_specs=(pl.BlockSpec(memory_space=pltpu.HBM),) * 2,
        scratch_shapes=[pltpu.SemaphoreType.DMA((quarters, 2))],
        compiler_params=vmem(10),
        name="assemble",
    )(*parts)


def solution(mesh):
    return jax.shard_map(
        shards,
        mesh=mesh,
        in_specs=(
            P("mem", "cell"),
            P("mem", "cell"),
            P("cell"),
            P(None, "cell"),
            P("cell"),
            P("cell", None),
            P("cell", None),
            P("cell", None),
        ),
        out_specs=(P("mem", "cell"), P("mem", "cell")),
        check_vma=False,
    )
```

time: 210 us -> 101 us (0.48)
  the two profiles are of different devices: /device:TPU:2 before, /device:TPU:1 now
where the time goes in v1:
time: 101 us
  waiting for transfers between devices  33.4 us (33%)
  starting transfers between devices  29.9 us (30%)
  Pallas kernels  27.4 us (27%)
  blocking collectives  8.8 us (9%)
    ppermute x6, waiting for transfers between devices, turned(): lax.ppermute(x, 'mem', [(i, (i + by) % quarters) for i in range(quarters)])  24.2 us
    all_to_all x1, starting transfers between devices, shards(): lax.all_to_all(totals, 'cell', split_axis=0, concat_axis=0, tiled=True)  13.4 us
    pallas_call x1, Pallas kernels, shards(): pl.pallas_call(functools.partial(transform_kernel, total_obs=float(obs *...  13.1 us
    pallas_call x1, Pallas kernels, shards(): pl.pallas_call(forecast_kernel, out_shape=(block,) * quarters + (jax.Shap...  9.61 us
    all_to_all x1, blocking collectives, shards(): lax.all_to_all(seen, 'mem', split_axis=0, concat_axis=0, tiled=True)  8.8 us
    ppermute x6, starting transfers between devices, turned(): lax.ppermute(x, 'mem', [(i, (i + by) % quarters) for i in range(quarters)])  6.05 us
    ppermute x1, starting transfers between devices, shards(): low = lax.ppermute(ends[0], 'cell', up)  5.04 us
    all_to_all x1, waiting for transfers between devices, shards(): lax.all_to_all(totals, 'cell', split_axis=0, concat_axis=0, tiled=True)  4.73 us
  transfers between devices with their start and end apart: 10, of which 6 were waited for; matrix products, arithmetic and copies ran while one was open for 0% of the time, Pallas kernels for 13%

profile of v1, /device:TPU:1, one launch (start us, length us, event | category | flops | bytes accessed | tf_op | source)
XLA Modules:
  0.0 101.0 jit_solution(8363023713811374721)
XLA Ops:
  0.6 0.0 copy-start
  0.6 0.0 copy-start.1
  0.7 0.0 copy-start.2
  0.7 0.0 copy-start.3
  0.7 0.0 copy-start.4
  0.7 1.5 %message.1 = (f32[40,128]{1,0:T(8,128)}, f32[40,128]{1,0:T(8,128)}) custom-call(f32[16,16384]{1,0:T(8,128)} %depth.1, f32[16,16384]{1,0:T(8,128)} %flow.1, s32[1,16384]{1,0:T(1,128)} %bitcast.7, s32[2,16384]{1,0:T(2,128)} %pump.1, f32[1,16384]{1,0:T(1,128)} %bitcast.10, f32[16,16384]{1,0:T(8,128)} %depth.1, f32[16,16384]{1,0:T(8,128)} %flow.1, ...), custom_call_target="tpu_custom_call" | custom-call | tf_op jit(solution)/shard_map/message/pallas_call | solution.py:325
  2.2 0.0 copy-start.5
  2.2 5.0 %collective-permute-start = (f32[40,128]{1,0:T(8,128)}, f32[40,128]{1,0:T(8,128)S(1)}, u32[]{:S(2)}, u32[]{:S(2)}) collective-permute-start(f32[40,128]{1,0:T(8,128)} %get-tuple-element.18), channel_id=1, source_target_pairs={{0,1},{1,2},{2,3},{3,4},{4,5},{5,6},{6,7},{7,8},{8,9},{9,10},{10,1... | collective-permute-start | bytes 61448 | tf_op jit(solution)/shard_map/ppermute | solution.py:335
  7.3 1.9 %collective-permute-start.1 = (f32[40,128]{1,0:T(8,128)}, f32[40,128]{1,0:T(8,128)S(1)}, u32[]{:S(2)}, u32[]{:S(2)}) collective-permute-start(f32[40,128]{1,0:T(8,128)} %get-tuple-element.19), channel_id=1, source_target_pairs={{1,0},{2,1},{3,2},{4,3},{5,4},{6,5},{7,6},{8,7},{9,8},{10,9},{11,1... | collective-permute-start | bytes 61448 | tf_op jit(solution)/shard_map/ppermute | solution.py:336
  9.2 0.0 collective-permute-done.low
  9.2 3.4 %collective-permute-done.1.high = f32[40,128]{1,0:T(8,128)S(1)} collective-permute-done((f32[40,128]{1,0:T(8,128)}, f32[40,128]{1,0:T(8,128)S(1)}, u32[]{:S(2)}, u32[]{:S(2)}) %collective-permute-start.1) | collective-permute-done | bytes 20512 | tf_op jit(solution)/shard_map/ppermute | solution.py:336
  12.6 0.0 copy-done
  12.6 0.0 copy-done.1
  12.6 0.0 copy-done.2
  12.6 0.0 copy-done.3
  12.6 0.0 copy-done.4
  12.6 0.0 copy-done.5
  12.6 9.6 %forecast.1 = (f32[2,16,4096]{2,1,0:T(8,128)S(1)}, f32[2,16,4096]{2,1,0:T(8,128)S(1)}, f32[2,16,4096]{2,1,0:T(8,128)}, f32[2,16,4096]{2,1,0:T(8,128)}, f32[4,16,512]{2,1,0:T(8,128)S(1)}) custom-call(f32[16,16384]{1,0:T(8,128)S(1)} %copy-done, f32[16,16384]{1,0:T(8,128)S(1)} %copy-done.1, s32[1,16384]{1,0:T(1,128)S(1)} %bitcast.9, s32[2,16384]{1,0:T(2,128)S(1)} %copy-done.2, ...), custom_call_target="tpu_custom_call" | custom-call | tf_op jit(solution)/shard_map/forecast/pallas_call | solution.py:339
  22.2 8.8 %all_to_all.16.seen = f32[4,16,512]{2,1,0:T(8,128)S(1)} all-to-all(f32[4,16,512]{2,1,0:T(8,128)S(1)} %get-tuple-element.21), channel_id=1, replica_groups=mesh['mem'=4,'cell'=64] {'mem'}, dimensions={0} | all-to-all | bytes 262144 | tf_op jit(solution)/shard_map/all_to_all | solution.py:349
  31.0 0.0 copy-start.7
  31.0 0.0 copy-start.6
  31.0 0.7 copy-done.7
  31.7 0.0 copy-done.6
  31.7 0.9 totals.1
  32.6 0.3 collective-permute-start.2
  32.9 1.8 %collective-permute-start.3 = (f32[2,16,4096]{2,1,0:T(8,128)}, f32[2,16,4096]{2,1,0:T(8,128)S(1)}, u32[]{:S(2)}, u32[]{:S(2)}) collective-permute-start(f32[2,16,4096]{2,1,0:T(8,128)} %get-tuple-element.26), channel_id=1, source_target_pairs={{0,128},{64,192},{128,0},{192,64},{1,129},{65,193},{129,1},{193,65... | collective-permute-start | bytes 1572872 | tf_op jit(solution)/shard_map/ppermute | solution.py:365
  34.7 0.6 collective-permute-start.4
  35.3 13.4 %all-to-all-start.1 = ((f32[64,1,128]{2,1,0:T(1,128)}), f32[64,1,128]{2,1,0:T(1,128)S(1)}, u32[]{:S(2)}, u32[]{:S(2)}) async-start(f32[64,1,128]{2,1,0:T(1,128)} %bitcast.4), calls=%async_computation.1 | async-start | bytes 65536 | tf_op jit(solution)/shard_map/all_to_all | solution.py:372
  48.7 3.5 %collective-permute-start.5 = (f32[72,64]{1,0:T(8,128)S(1)}, f32[72,64]{1,0:T(8,128)S(1)}, u32[]{:S(2)}, u32[]{:S(2)}) collective-permute-start(f32[72,64]{1,0:T(8,128)S(1)} %get-tuple-element.29), channel_id=1, source_target_pairs={{0,1},{1,2},{2,3},{3,4},{4,5},{5,6},{6,7},{7,8},{8,9},{9,10},{10,1... | collective-permute-start | bytes 55304 | tf_op jit(solution)/shard_map/ppermute | solution.py:371
  52.2 1.0 %collective-permute-done.5.edge = f32[72,64]{1,0:T(8,128)S(1)} collective-permute-done((f32[72,64]{1,0:T(8,128)S(1)}, f32[72,64]{1,0:T(8,128)S(1)}, u32[]{:S(2)}, u32[]{:S(2)}) %collective-permute-start.5) | collective-permute-done | bytes 18464 | tf_op jit(solution)/shard_map/ppermute | solution.py:371
  53.3 4.7 %all-to-all-done.1 = f32[64,1,128]{2,1,0:T(1,128)S(1)} async-done(((f32[64,1,128]{2,1,0:T(1,128)}), f32[64,1,128]{2,1,0:T(1,128)S(1)}, u32[]{:S(2)}, u32[]{:S(2)}) %all-to-all-start.1) | async-done | bytes 32800 | tf_op jit(solution)/shard_map/all_to_all | solution.py:372
  58.0 13.1 %transform.1.refs_4_ = f32[2,64,256]{2,1,0:T(8,128)S(1)} custom-call(f32[4,16,512]{2,1,0:T(8,128)S(1)} %all_to_all.16.seen, f32[1,512]{1,0:T(1,128)S(1)} %copy-done.6, f32[1,512]{1,0:T(1,128)S(1)} %copy-done.7, s32[1,512]{1,0:T(1,128)S(1)} %copy-done.5, f32[64,128]{1,0:T(8,128)S(1)} %bitcast.13, f32[72,64]{1,0:T(8,128)S(1)} %collective-permute-done.5.edge), custom_call_target="tpu_custom_call" | custom-call | tf_op jit(solution)/shard_map/transform/pallas_call | solution.py:374
  71.1 0.0 collective-permute-done.2.refs_1_
  71.1 0.0 collective-permute-done.3.refs_2_
  71.1 0.0 collective-permute-done.4.refs_3_
  71.1 0.9 apply.1
  72.1 1.0 collective-permute-start.6
  73.1 1.8 %collective-permute-start.7 = (f32[2,16,4096]{2,1,0:T(8,128)S(1)}, f32[2,16,4096]{2,1,0:T(8,128)S(1)}, u32[]{:S(2)}, u32[]{:S(2)}) collective-permute-start(f32[2,16,4096]{2,1,0:T(8,128)S(1)} %get-tuple-element.32), channel_id=1, source_target_pairs={{0,128},{64,192},{128,0},{192,64},{1,129},{65,193},{129,1},{193,65... | collective-permute-start | bytes 1572872 | tf_op jit(solution)/shard_map/ppermute | solution.py:365
  74.9 0.6 collective-permute-start.8
  75.5 9.5 %collective-permute-done.6.refs_1_ = f32[2,16,4096]{2,1,0:T(8,128)S(1)} collective-permute-done((f32[2,16,4096]{2,1,0:T(8,128)S(1)}, f32[2,16,4096]{2,1,0:T(8,128)S(1)}, u32[]{:S(2)}, u32[]{:S(2)}) %collective-permute-start.6) | collective-permute-done | bytes 524320 | tf_op jit(solution)/shard_map/ppermute | solution.py:365
  85.0 2.2 %collective-permute-done.7.refs_2_ = f32[2,16,4096]{2,1,0:T(8,128)S(1)} collective-permute-done((f32[2,16,4096]{2,1,0:T(8,128)S(1)}, f32[2,16,4096]{2,1,0:T(8,128)S(1)}, u32[]{:S(2)}, u32[]{:S(2)}) %collective-permute-start.7) | collective-permute-done | bytes 524320 | tf_op jit(solution)/shard_map/ppermute | solution.py:365
  87.2 12.5 %collective-permute-done.8.refs_3_ = f32[2,16,4096]{2,1,0:T(8,128)S(1)} collective-permute-done((f32[2,16,4096]{2,1,0:T(8,128)S(1)}, f32[2,16,4096]{2,1,0:T(8,128)S(1)}, u32[]{:S(2)}, u32[]{:S(2)}) %collective-permute-start.8) | collective-permute-done | bytes 524320 | tf_op jit(solution)/shard_map/ppermute | solution.py:365
  99.7 1.4 %assemble.1 = (f32[16,16384]{1,0:T(8,128)}, f32[16,16384]{1,0:T(8,128)}) custom-call(f32[2,16,4096]{2,1,0:T(8,128)S(1)} %get-tuple-element.30.refs_0_, f32[2,16,4096]{2,1,0:T(8,128)S(1)} %collective-permute-done.6.refs_1_, f32[2,16,4096]{2,1,0:T(8,128)S(1)} %collective-permute-done.7.refs_2_, f32[2,16,4096]{2,1,0:T(8,128)S(1)} %collective-permute-done.8.refs_3_), custom_call_target="tpu_custom_call" | custom-call | tf_op jit(solution)/shard_map/assemble/pallas_call | solution.py:393
Async XLA Ops:
  0.6 12.0 %copy-start = (f32[16,16384]{1,0:T(8,128)S(1)}, f32[16,16384]{1,0:T(8,128)}, u32[]{:S(2)}) copy-start(f32[16,16384]{1,0:T(8,128)} %depth.1) | copy-start | bytes 3145732
  0.6 12.0 %copy-start.1 = (f32[16,16384]{1,0:T(8,128)S(1)}, f32[16,16384]{1,0:T(8,128)}, u32[]{:S(2)}) copy-start(f32[16,16384]{1,0:T(8,128)} %flow.1) | copy-start | bytes 3145732
  0.7 11.9 %copy-start.2 = (s32[2,16384]{1,0:T(2,128)S(1)}, s32[2,16384]{1,0:T(2,128)}, u32[]{:S(2)}) copy-start(s32[2,16384]{1,0:T(2,128)} %pump.1) | copy-start | bytes 393220
  0.7 11.9 %copy-start.3 = (s32[16384]{0:T(1024)S(1)}, s32[16384]{0:T(1024)}, u32[]{:S(2)}) copy-start(s32[16384]{0:T(1024)} %param.10) | copy-start | bytes 196612
  0.7 11.9 %copy-start.4 = (f32[16384]{0:T(1024)S(1)}, f32[16384]{0:T(1024)}, u32[]{:S(2)}) copy-start(f32[16384]{0:T(1024)} %param.12) | copy-start | bytes 196612
  2.2 10.4 %copy-start.5 = (s32[1,512]{1,0:T(1,128)S(1)}, s32[1,512]{1,0:T(1,128)}, u32[]{:S(2)}) copy-start(s32[1,512]{1,0:T(1,128)} %offsets.3) | copy-start | bytes 6148
  2.2 7.0 %collective-permute-start = (f32[40,128]{1,0:T(8,128)}, f32[40,128]{1,0:T(8,128)S(1)}, u32[]{:S(2)}, u32[]{:S(2)}) collective-permute-start(f32[40,128]{1,0:T(8,128)} %get-tuple-element.18), channel_id=1, source_target_pairs={{0,1},{1,2},{2,3},{3,4},{4,5},{5,6},{6,7},{7,8},{8,9},{9,10},{10,1... | collective-permute-start | bytes 61448 | tf_op jit(solution)/shard_map/ppermute | solution.py:335
  7.3 5.3 %collective-permute-start.1 = (f32[40,128]{1,0:T(8,128)}, f32[40,128]{1,0:T(8,128)S(1)}, u32[]{:S(2)}, u32[]{:S(2)}) collective-permute-start(f32[40,128]{1,0:T(8,128)} %get-tuple-element.19), channel_id=1, source_target_pairs={{1,0},{2,1},{3,2},{4,3},{5,4},{6,5},{7,6},{8,7},{9,8},{10,9},{11,1... | collective-permute-start | bytes 61448 | tf_op jit(solution)/shard_map/ppermute | solution.py:336
  31.0 0.7 copy-start.7
  31.0 0.7 copy-start.6
  32.6 38.5 %collective-permute-start.2 = (f32[2,16,4096]{2,1,0:T(8,128)S(1)}, f32[2,16,4096]{2,1,0:T(8,128)S(1)}, u32[]{:S(2)}, u32[]{:S(2)}) collective-permute-start(f32[2,16,4096]{2,1,0:T(8,128)S(1)} %get-tuple-element.25), channel_id=1, source_target_pairs={{0,64},{64,128},{128,192},{192,0},{1,65},{65,129},{129,193},{193,1... | collective-permute-start | bytes 1572872 | tf_op jit(solution)/shard_map/ppermute | solution.py:365
  32.9 38.2 %collective-permute-start.3 = (f32[2,16,4096]{2,1,0:T(8,128)}, f32[2,16,4096]{2,1,0:T(8,128)S(1)}, u32[]{:S(2)}, u32[]{:S(2)}) collective-permute-start(f32[2,16,4096]{2,1,0:T(8,128)} %get-tuple-element.26), channel_id=1, source_target_pairs={{0,128},{64,192},{128,0},{192,64},{1,129},{65,193},{129,1},{193,65... | collective-permute-start | bytes 1572872 | tf_op jit(solution)/shard_map/ppermute | solution.py:365
  34.7 36.5 %collective-permute-start.4 = (f32[2,16,4096]{2,1,0:T(8,128)}, f32[2,16,4096]{2,1,0:T(8,128)S(1)}, u32[]{:S(2)}, u32[]{:S(2)}) collective-permute-start(f32[2,16,4096]{2,1,0:T(8,128)} %get-tuple-element.27), channel_id=1, source_target_pairs={{0,192},{64,0},{128,64},{192,128},{1,193},{65,1},{129,65},{193,129... | collective-permute-start | bytes 1572872 | tf_op jit(solution)/shard_map/ppermute | solution.py:365
  35.3 22.7 %all-to-all-start.1 = ((f32[64,1,128]{2,1,0:T(1,128)}), f32[64,1,128]{2,1,0:T(1,128)S(1)}, u32[]{:S(2)}, u32[]{:S(2)}) async-start(f32[64,1,128]{2,1,0:T(1,128)} %bitcast.4), calls=%async_computation.1 | async-start | bytes 65536 | tf_op jit(solution)/shard_map/all_to_all | solution.py:372
  48.7 4.6 %collective-permute-start.5 = (f32[72,64]{1,0:T(8,128)S(1)}, f32[72,64]{1,0:T(8,128)S(1)}, u32[]{:S(2)}, u32[]{:S(2)}) collective-permute-start(f32[72,64]{1,0:T(8,128)S(1)} %get-tuple-element.29), channel_id=1, source_target_pairs={{0,1},{1,2},{2,3},{3,4},{4,5},{5,6},{6,7},{7,8},{8,9},{9,10},{10,1... | collective-permute-start | bytes 55304 | tf_op jit(solution)/shard_map/ppermute | solution.py:371
  72.1 12.9 %collective-permute-start.6 = (f32[2,16,4096]{2,1,0:T(8,128)S(1)}, f32[2,16,4096]{2,1,0:T(8,128)S(1)}, u32[]{:S(2)}, u32[]{:S(2)}) collective-permute-start(f32[2,16,4096]{2,1,0:T(8,128)S(1)} %get-tuple-element.31), channel_id=1, source_target_pairs={{0,192},{64,0},{128,64},{192,128},{1,193},{65,1},{129,65},{193,129... | collective-permute-start | bytes 1572872 | tf_op jit(solution)/shard_map/ppermute | solution.py:365
  73.1 14.1 %collective-permute-start.7 = (f32[2,16,4096]{2,1,0:T(8,128)S(1)}, f32[2,16,4096]{2,1,0:T(8,128)S(1)}, u32[]{:S(2)}, u32[]{:S(2)}) collective-permute-start(f32[2,16,4096]{2,1,0:T(8,128)S(1)} %get-tuple-element.32), channel_id=1, source_target_pairs={{0,128},{64,192},{128,0},{192,64},{1,129},{65,193},{129,1},{193,65... | collective-permute-start | bytes 1572872 | tf_op jit(solution)/shard_map/ppermute | solution.py:365
  74.9 24.8 %collective-permute-start.8 = (f32[2,16,4096]{2,1,0:T(8,128)S(1)}, f32[2,16,4096]{2,1,0:T(8,128)S(1)}, u32[]{:S(2)}, u32[]{:S(2)}) collective-permute-start(f32[2,16,4096]{2,1,0:T(8,128)S(1)} %get-tuple-element.33), channel_id=1, source_target_pairs={{0,64},{64,128},{128,192},{192,0},{1,65},{65,129},{129,193},{193,1... | collective-permute-start | bytes 1572872 | tf_op jit(solution)/shard_map/ppermute | solution.py:365

commit v2 on v1

--- a/solution.py
+++ b/solution.py
@@ -8,6 +8,8 @@
 
 PER = 512
 NS_ITERS = 12
+FULL_ITERS = 6
+PACK = 4
 gravity = 9.81
 step_dt = 0.06
 LANE = 128
@@ -34,9 +36,9 @@
     b = jnp.maximum(jnp.maximum(pltpu.roll(fast, 1, 1), fast), 0.0)
     ml = pltpu.roll(moment, 1, 1)
     inv = 1.0 / (b - a)
-    ab = a * b
-    mass = (b * ql - a * q + ab * (h - hl)) * inv
-    mom = (b * ml - a * moment + ab * (q - ql)) * inv
+    share = a * inv
+    mass = ql - share * ((q - ql) - b * (h - hl))
+    mom = ml - share * ((moment - ml) - b * (q - ql))
     opened = jnp.broadcast_to(gate, h.shape) > 0.5
     opened_next = jnp.broadcast_to(pltpu.roll(gate, back, 1), h.shape) > 0.5
     mass = jnp.where(opened, mass, 0.0)
@@ -48,9 +50,12 @@
 
 
 def forecast_kernel(
-    depth, flow, gate, pump, rate, low, high, offsets, *refs
+    depth, flow, gate, pump, rate, low, high, value, error, offsets, *refs
 ):
-    *fields, seen, h0, q0, h1, q1, rows, table = refs
+    *fields, seen, obs_rows, h0, q0, h1, q1, rows, table = refs
+    obs_rows[0:1] = value[...]
+    obs_rows[1:2] = 1.0 / error[...]
+    obs_rows[2:] = jnp.zeros((6, value.shape[1]), F32)
     members, cells = depth.shape
     quarters = len(fields)
     quart = cells // quarters
@@ -79,7 +84,7 @@
     shut = jnp.where(first, 1, 0) * jnp.where(lane == 0, 1, 0)
     rows[0:1, pad : pad + LANE] = jnp.where(shut > 0, 0.0, rows[0:1, pad : pad + LANE])
 
-    w1 = 26 * LANE
+    w1 = 65 * LANE
 
     def first_step(i, _):
         at = pl.ds(pl.multiple_of(i * w1, LANE), w1 + 2 * LANE)
@@ -90,7 +95,7 @@
         return 0
 
     lax.fori_loop(0, (cells + 2 * LANE) // w1, first_step, 0)
-    w2 = 16 * LANE
+    w2 = 32 * LANE
     for k in range(quarters):
         first_tile = lax.rem(lax.axis_index("mem") + k, quarters) * (quart // LANE)
 
@@ -135,18 +140,19 @@
         out[2 * n + 2 :] = jnp.zeros((6, LANE), F32)
 
 
-def scaled_obs(seen_ref, value, error):
+def scaled_obs(seen_ref, obs_rows):
     groups = seen_ref.shape[0]
     mem = lax.axis_index("mem")
     seen = jnp.concatenate([seen_ref[lax.rem(mem + groups - k, groups)] for k in range(groups)], axis=0)
     mean = jnp.mean(seen, axis=0, keepdims=True)
-    precision = 1.0 / error
+    value = obs_rows[0:1]
+    precision = obs_rows[1:2]
     return (seen - mean) * precision, (value - mean) * precision
 
 
-def totals_kernel(seen, value, error, offsets, *refs, last):
+def totals_kernel(seen, obs_rows, offsets, *refs, last):
     totals, edge = refs[3:5]
-    scaled, innov = scaled_obs(seen, value[...], error[...])
+    scaled, innov = scaled_obs(seen, obs_rows)
     members = scaled.shape[0]
     misfit = jnp.sum(innov * innov, axis=(0, 1), keepdims=True)
     spread = jnp.sum(scaled * scaled, axis=(0, 1), keepdims=True) / (members - 1)
@@ -170,16 +176,20 @@
     return lax.dot_general(a, b, (((1,), (0,)), ((), ())), preferred_element_type=F32)
 
 
-def transform_kernel(seen, value, error, offsets, totals, edge, mixing, weights, *, total_obs):
-    scaled, innov = scaled_obs(seen, value[...], error[...])
-    members = scaled.shape[0]
-    pack = 4
+def gram_kernel(seen, obs_rows, offsets, grams):
+    groups = grams.shape[0]
+    scaled, innov = scaled_obs(seen, obs_rows)
+    extended = jnp.concatenate([scaled, jnp.broadcast_to(innov, (8, innov.shape[1]))], axis=0)
+    polder = offsets[...] // PER - lax.axis_index("mem") * (groups * PACK)
+    for g in range(groups):
+        picked = [jnp.where(jnp.abs(polder - (g * PACK + k)) <= 1, scaled, 0.0) for k in range(PACK)]
+        grams[g] = mm(extended, jnp.concatenate(picked, axis=0), ((1,), (1,)))
+
+
+def transform_kernel(grams, totals, edge, mixing, weights, *, total_obs):
     groups = mixing.shape[0]
-    wide = pack * members
+    members, wide = mixing.shape[1:]
     weights[...] = jnp.zeros(weights.shape, BF16)
-    extended = jnp.concatenate([scaled, jnp.broadcast_to(innov, (8, innov.shape[1]))], axis=0)
-    mem = lax.axis_index("mem")
-    polder = offsets[...] // PER - mem * (groups * pack)
     sums = jnp.sum(totals[...], axis=0, keepdims=True)
     lane = lax.broadcasted_iota(jnp.int32, sums.shape, 1)
     misfit = jnp.sum(jnp.where(lane == 0, sums, 0.0), axis=(0, 1), keepdims=True)
@@ -189,67 +199,66 @@
     r64 = lax.broadcasted_iota(jnp.int32, (members, wide), 0)
     c64 = lax.broadcasted_iota(jnp.int32, (members, wide), 1)
     eye = jnp.where(r64 == c64 % members, 1.0, 0.0)
-    half = lax.broadcasted_iota(jnp.int32, (members, LANE), 1) // members
-    keep = [jnp.where(half == k, 1.0, 0.0).astype(BF16) for k in range(2)]
+    keep = [jnp.where(c64 // members == k, 1.0, 0.0).astype(BF16) for k in range(PACK)]
 
     def load_weights(g, parts):
         for p, part in enumerate(parts):
-            for k in range(pack):
+            for k in range(PACK):
                 cols = slice((k // 2) * LANE, (k // 2 + 1) * LANE)
-                weights[g, p, k * members : (k + 1) * members, cols] = part[:, cols] * keep[k % 2]
-
-    def product(g, pieces):
+                row = p * wide + k * members
+                weights[g, row : row + members, cols] = part[:, cols] * keep[k][:, cols]
+
+    def product(g, pieces, full=True):
         n = [p[0].shape[0] for p in pieces]
         total = [None] * len(pieces)
-        for w, depth in ((2, 1), (1, 2), (0, 3)):
+        for w, depth in ((2, 1), (1, 2), (0, 3)) if full else ((1, 1), (0, 2)):
             stack = jnp.concatenate([p[d] for p in pieces for d in range(depth)], axis=0)
-            y = dot(stack, weights[g, w])
+            y = dot(stack, weights[g, w * wide : (w + 1) * wide])
             at = 0
             for i in range(len(pieces)):
-                slabs = [y[at + d * n[i] : at + (d + 1) * n[i]] for d in range(depth)]
+                piece = y[at + (depth - 1) * n[i] : at + depth * n[i]]
+                for d in reversed(range(depth - 1)):
+                    piece = piece + y[at + d * n[i] : at + (d + 1) * n[i]]
                 at += depth * n[i]
-                piece = slabs[-1]
-                for z in reversed(slabs[:-1]):
-                    piece = piece + z
                 total[i] = piece if total[i] is None else total[i] + piece
         return total
 
+    mem = lax.axis_index("mem")
     low_edge = jnp.where(mem == 0, 1.0, 0.0)
     high_edge = jnp.where(mem == lax.axis_size("mem") - 1, 1.0, 0.0)
-    wide_edge = jnp.concatenate([edge[...]] * pack, axis=1)
+    wide_edge = jnp.concatenate([edge[...]] * PACK, axis=1)
     e_col = lax.broadcasted_iota(jnp.int32, wide_edge.shape, 1) // members
     starts = []
     for g in range(groups):
-        picked = jnp.concatenate(
-            [jnp.where(jnp.abs(polder - (g * pack + k)) <= 1, scaled, 0.0) for k in range(pack)], axis=0
-        )
-        gram = mm(extended, picked, ((1,), (1,)))
+        gram = grams[g]
         if g == 0:
             gram = gram + jnp.where(e_col == 0, wide_edge * low_edge, 0.0)
         if g == groups - 1:
-            gram = gram + jnp.where(e_col == pack - 1, wide_edge * high_edge, 0.0)
+            gram = gram + jnp.where(e_col == PACK - 1, wide_edge * high_edge, 0.0)
         system = eye + rho2 / (members - 1) * gram[:members]
         squares = jnp.sum(system * system, axis=0, keepdims=True)
         column = lax.broadcasted_iota(jnp.int32, squares.shape, 1) // members
         norm2 = jnp.zeros_like(squares)
-        for k in range(pack):
+        for k in range(PACK):
             here = jnp.where(column == k, squares, 0.0)
             norm2 = jnp.where(column == k, jnp.sum(here, axis=1, keepdims=True), norm2)
         norm = jnp.sqrt(norm2)
         starts.append((system / norm, gram[members : members + 8], norm))
 
-    def iterate(turn, carry):
+    def iterate(full, turn, carry):
         out = []
         for g in range(groups):
             energy, inverse = carry[g]
             parts = split(energy)
             load_weights(g, parts)
-            square, step = product(g, [parts, split(inverse)])
+            square, step = product(g, [parts, split(inverse)], full)
             factor = 2.25 * eye - 1.5 * energy + 0.25 * square
-            out.append((product(g, [split(factor)])[0], 1.5 * inverse - 0.5 * step))
+            out.append((product(g, [split(factor)], full)[0], 1.5 * inverse - 0.5 * step))
         return tuple(out)
 
-    carry = lax.fori_loop(0, NS_ITERS, iterate, tuple((s[0], eye) for s in starts))
+    carry = tuple((s[0], eye) for s in starts)
+    carry = lax.fori_loop(0, FULL_ITERS, functools.partial(iterate, True), carry)
+    carry = lax.fori_loop(FULL_ITERS, NS_ITERS, functools.partial(iterate, False), carry)
     for g in range(groups):
         _, cross, norm = starts[g]
         inverse = carry[g][1]
@@ -265,7 +274,7 @@
     _, rows, width = fields[0].shape
     members = quarters * rows
     for u in range(width // PER):
-        mix = mixing[u // 4, :, (u % 4) * members : (u % 4 + 1) * members]
+        mix = mixing[u // PACK, :, (u % PACK) * members : (u % PACK + 1) * members]
         mix_hi = mix.astype(BF16)
         mix_lo = (mix - mix_hi.astype(F32)).astype(BF16)
         left = jnp.concatenate([mix_hi, mix_hi, mix_lo, mix_lo], axis=1)
@@ -336,16 +345,16 @@
     high = lax.ppermute(ends[1], "cell", down)
     total = cells + 4 * LANE
     block = jax.ShapeDtypeStruct((2, rows, quart), F32)
-    own, *sent, seen = pl.pallas_call(
+    own, *sent, seen, obs_rows = pl.pallas_call(
         forecast_kernel,
-        out_shape=(block,) * quarters + (jax.ShapeDtypeStruct((quarters, rows, obs), F32),),
-        in_specs=[VM] * 7 + [SM],
-        out_specs=(VM,) * (quarters + 1),
+        out_shape=(block,) * quarters + (jax.ShapeDtypeStruct((quarters, rows, obs), F32), jax.ShapeDtypeStruct((8, obs), F32)),
+        in_specs=[VM] * 9 + [SM],
+        out_specs=(VM,) * (quarters + 2),
         scratch_shapes=[pltpu.VMEM((rows, total), F32)] * 4
         + [pltpu.VMEM((8, total), F32), pltpu.VMEM((cells // LANE, rows, LANE), F32)],
         compiler_params=vmem(24),
         name="forecast",
-    )(depth, discharge, gate_row, pump, rate_row, low, high, obs_index.reshape(obs))
+    )(depth, discharge, gate_row, pump, rate_row, low, high, obs_value, obs_error, obs_index.reshape(obs))
     seen_all = lax.all_to_all(seen, "mem", split_axis=0, concat_axis=0, tiled=True)
     totals, edge, *sent = pl.pallas_call(
         functools.partial(totals_kernel, last=cells // PER - 1),
@@ -354,12 +363,12 @@
             jax.ShapeDtypeStruct((members + 8, members), F32),
         )
         + (block,) * 3,
-        in_specs=[VM, VM, VM, VM, ANY, ANY, ANY],
+        in_specs=[VM, VM, VM, ANY, ANY, ANY],
         out_specs=(VM, VM, ANY, ANY, ANY),
-        input_output_aliases={4: 2, 5: 3, 6: 4},
+        input_output_aliases={3: 2, 4: 3, 5: 4},
         compiler_params=vmem(8),
         name="totals",
-    )(seen_all, obs_value, obs_error, obs_index, *sent)
+    )(seen_all, obs_rows, obs_index, *sent)
 
     def turned(x, by):
         return lax.ppermute(x, "mem", [(i, (i + by) % quarters) for i in range(quarters)])
@@ -370,16 +379,25 @@
     pairs += [(top * slabs + i + 1, top * slabs + i) for i in range(slabs - 1)]
     edge = lax.ppermute(edge, ("mem", "cell"), pairs)
     everyone = lax.all_to_all(totals, "cell", split_axis=0, concat_axis=0, tiled=True)
-    groups = quart // PER // 4
+    groups = quart // PER // PACK
+    wide = PACK * members
+    grams = pl.pallas_call(
+        gram_kernel,
+        out_shape=jax.ShapeDtypeStruct((groups, members + 8, wide), F32),
+        in_specs=[VM] * 3,
+        out_specs=VM,
+        compiler_params=vmem(10),
+        name="gram",
+    )(seen_all, obs_rows, obs_index)
     mixing = pl.pallas_call(
         functools.partial(transform_kernel, total_obs=float(obs * slabs)),
-        out_shape=jax.ShapeDtypeStruct((groups, members, 4 * members), F32),
-        in_specs=[VM] * 6,
+        out_shape=jax.ShapeDtypeStruct((groups, members, wide), F32),
+        in_specs=[VM] * 3,
         out_specs=VM,
-        scratch_shapes=[pltpu.VMEM((groups, 3, 4 * members, 4 * members), BF16)],
+        scratch_shapes=[pltpu.VMEM((groups, 3 * wide, wide), BF16)],
         compiler_params=vmem(12),
         name="transform",
-    )(seen_all, obs_value, obs_error, obs_index, everyone, edge)
+    )(grams, everyone, edge)
     kept, *given = pl.pallas_call(
         apply_kernel,
         out_shape=(block,) * quarters,

time: 101 us -> 97.4 us (0.964)
  Pallas kernels: 27.4 us -> 25.3 us
  waiting for transfers between devices: 33.4 us -> 32.2 us
    pallas_call x1, Pallas kernels: 13.1 us -> 10.3 us  [shards(): pl.pallas_call(functools.partial(transform_kernel, total_obs=float(obs *...]
    pallas_call x0 -> x1, Pallas kernels: none -> 1.14 us  [shards(): pl.pallas_call(gram_kernel, out_shape=jax.ShapeDtypeStruct((groups, membe...]
    ppermute x1, waiting for transfers between devices: 1.04 us -> 0.01 us  [shards(): edge = lax.ppermute(edge, ('mem', 'cell'), pairs)]
  transfers between devices with their start and end apart: 10 -> 10, of which waited for: 6 -> 5; matrix products, arithmetic and copies ran while one was open for 0% -> 0% of each run, Pallas kernels for 13% -> 12%
where the time goes in v2:
time: 97.4 us; the launch traced here: 97.1 us
  waiting for transfers between devices  32.2 us (33%)
  starting transfers between devices  29.9 us (31%)
  Pallas kernels  25.3 us (26%)
  blocking collectives  8.8 us (9%)
    ppermute x6, waiting for transfers between devices, turned(): lax.ppermute(x, 'mem', [(i, (i + by) % quarters) for i in range(quarters)])  24.2 us
    all_to_all x1, starting transfers between devices, shards(): lax.all_to_all(totals, 'cell', split_axis=0, concat_axis=0, tiled=True)  13.4 us
    pallas_call x1, Pallas kernels, shards(): pl.pallas_call(functools.partial(transform_kernel, total_obs=float(obs *...  10.3 us
    pallas_call x1, Pallas kernels, shards(): pl.pallas_call(forecast_kernel, out_shape=(block,) * quarters + (jax.Shap...  9.11 us
    all_to_all x1, blocking collectives, shards(): lax.all_to_all(seen, 'mem', split_axis=0, concat_axis=0, tiled=True)  8.8 us
    ppermute x6, starting transfers between devices, turned(): lax.ppermute(x, 'mem', [(i, (i + by) % quarters) for i in range(quarters)])  6.04 us
    ppermute x1, starting transfers between devices, shards(): low = lax.ppermute(ends[0], 'cell', up)  5.05 us
    all_to_all x1, waiting for transfers between devices, shards(): lax.all_to_all(totals, 'cell', split_axis=0, concat_axis=0, tiled=True)  4.62 us
  transfers between devices with their start and end apart: 10, of which 5 were waited for; matrix products, arithmetic and copies ran while one was open for 0% of the time, Pallas kernels for 12%

profile of v2, /device:TPU:1, one launch (start us, length us, event | category | flops | bytes accessed | tf_op | source)
XLA Modules:
  0.0 97.1 jit_solution(18200426577051502996)
XLA Ops:
  0.6 0.0 copy-start
  0.6 0.0 copy-start.1
  0.7 0.0 copy-start.2
  0.7 0.0 copy-start.3
  0.7 0.0 copy-start.4
  0.7 0.0 copy-start.7
  0.7 1.5 %message.1 = (f32[40,128]{1,0:T(8,128)}, f32[40,128]{1,0:T(8,128)}) custom-call(f32[16,16384]{1,0:T(8,128)} %depth.1, f32[16,16384]{1,0:T(8,128)} %flow.1, s32[1,16384]{1,0:T(1,128)} %bitcast.7, s32[2,16384]{1,0:T(2,128)} %pump.1, f32[1,16384]{1,0:T(1,128)} %bitcast.10, f32[16,16384]{1,0:T(8,128)} %depth.1, f32[16,16384]{1,0:T(8,128)} %flow.1, ...), custom_call_target="tpu_custom_call" | custom-call | tf_op jit(solution)/shard_map/message/pallas_call | solution.py:334
  2.2 0.0 copy-start.6
  2.2 0.0 copy-start.5
  2.2 5.1 %collective-permute-start = (f32[40,128]{1,0:T(8,128)}, f32[40,128]{1,0:T(8,128)S(1)}, u32[]{:S(2)}, u32[]{:S(2)}) collective-permute-start(f32[40,128]{1,0:T(8,128)} %get-tuple-element.19), channel_id=1, source_target_pairs={{0,1},{1,2},{2,3},{3,4},{4,5},{5,6},{6,7},{7,8},{8,9},{9,10},{10,1... | collective-permute-start | bytes 61448 | tf_op jit(solution)/shard_map/ppermute | solution.py:344
  7.3 1.9 %collective-permute-start.1 = (f32[40,128]{1,0:T(8,128)}, f32[40,128]{1,0:T(8,128)S(1)}, u32[]{:S(2)}, u32[]{:S(2)}) collective-permute-start(f32[40,128]{1,0:T(8,128)} %get-tuple-element.20), channel_id=1, source_target_pairs={{1,0},{2,1},{3,2},{4,3},{5,4},{6,5},{7,6},{8,7},{9,8},{10,9},{11,1... | collective-permute-start | bytes 61448 | tf_op jit(solution)/shard_map/ppermute | solution.py:345
  9.2 0.0 collective-permute-done.low
  9.2 3.4 %collective-permute-done.1.high = f32[40,128]{1,0:T(8,128)S(1)} collective-permute-done((f32[40,128]{1,0:T(8,128)}, f32[40,128]{1,0:T(8,128)S(1)}, u32[]{:S(2)}, u32[]{:S(2)}) %collective-permute-start.1) | collective-permute-done | bytes 20512 | tf_op jit(solution)/shard_map/ppermute | solution.py:345
  12.6 0.0 copy-done
  12.6 0.0 copy-done.1
  12.6 0.0 copy-done.2
  12.6 0.0 copy-done.3
  12.6 0.0 copy-done.4
  12.6 0.0 copy-done.7
  12.6 0.0 copy-done.6
  12.6 0.0 copy-done.5
  12.6 9.1 %forecast.1 = (f32[2,16,4096]{2,1,0:T(8,128)S(1)}, f32[2,16,4096]{2,1,0:T(8,128)S(1)}, f32[2,16,4096]{2,1,0:T(8,128)}, f32[2,16,4096]{2,1,0:T(8,128)}, f32[4,16,512]{2,1,0:T(8,128)S(1)}, /*index=5*/f32[8,512]{1,0:T(8,128)S(1)}) custom-call(f32[16,16384]{1,0:T(8,128)S(1)} %copy-done, f32[16,16384]{1,0:T(8,128)S(1)} %copy-done.1, s32[1,16384]{1,0:T(1,128)S(1)} %bitcast.9, ...), custom_call_target="tpu_custom_call" | custom-call | tf_op jit(solution)/shard_map/forecast/pallas_call | solution.py:348
  21.8 8.8 %all_to_all.16.seen = f32[4,16,512]{2,1,0:T(8,128)S(1)} all-to-all(f32[4,16,512]{2,1,0:T(8,128)S(1)} %get-tuple-element.22), channel_id=1, replica_groups=mesh['mem'=4,'cell'=64] {'mem'}, dimensions={0} | all-to-all | bytes 262144 | tf_op jit(solution)/shard_map/all_to_all | solution.py:358
  30.6 0.9 totals.1
  31.4 0.3 collective-permute-start.2
  31.7 1.8 %collective-permute-start.3 = (f32[2,16,4096]{2,1,0:T(8,128)}, f32[2,16,4096]{2,1,0:T(8,128)S(1)}, u32[]{:S(2)}, u32[]{:S(2)}) collective-permute-start(f32[2,16,4096]{2,1,0:T(8,128)} %get-tuple-element.28), channel_id=1, source_target_pairs={{0,128},{64,192},{128,0},{192,64},{1,129},{65,193},{129,1},{193,65... | collective-permute-start | bytes 1572872 | tf_op jit(solution)/shard_map/ppermute | solution.py:374
  33.5 0.6 collective-permute-start.4
  34.1 13.4 %all-to-all-start.1 = ((f32[64,1,128]{2,1,0:T(1,128)}), f32[64,1,128]{2,1,0:T(1,128)S(1)}, u32[]{:S(2)}, u32[]{:S(2)}) async-start(f32[64,1,128]{2,1,0:T(1,128)} %bitcast.4), calls=%async_computation.1 | async-start | bytes 65536 | tf_op jit(solution)/shard_map/all_to_all | solution.py:381
  47.5 3.5 %collective-permute-start.5 = (f32[72,64]{1,0:T(8,128)S(1)}, f32[72,64]{1,0:T(8,128)S(1)}, u32[]{:S(2)}, u32[]{:S(2)}) collective-permute-start(f32[72,64]{1,0:T(8,128)S(1)} %get-tuple-element.31), channel_id=1, source_target_pairs={{0,1},{1,2},{2,3},{3,4},{4,5},{5,6},{6,7},{7,8},{8,9},{9,10},{10,1... | collective-permute-start | bytes 55304 | tf_op jit(solution)/shard_map/ppermute | solution.py:380
  51.0 1.1 %gram.1.grams = f32[2,72,256]{2,1,0:T(8,128)S(1)} custom-call(f32[4,16,512]{2,1,0:T(8,128)S(1)} %all_to_all.16.seen, f32[8,512]{1,0:T(8,128)S(1)} %get-tuple-element.23.obs_rows, s32[1,512]{1,0:T(1,128)S(1)} %copy-done.5), custom_call_target="tpu_custom_call" | custom-call | tf_op jit(solution)/shard_map/gram/pallas_call | solution.py:384
  52.2 0.0 collective-permute-done.5.edge
  52.2 4.6 %all-to-all-done.1 = f32[64,1,128]{2,1,0:T(1,128)S(1)} async-done(((f32[64,1,128]{2,1,0:T(1,128)}), f32[64,1,128]{2,1,0:T(1,128)S(1)}, u32[]{:S(2)}, u32[]{:S(2)}) %all-to-all-start.1) | async-done | bytes 32800 | tf_op jit(solution)/shard_map/all_to_all | solution.py:381
  56.8 10.3 %transform.1.refs_4_ = f32[2,64,256]{2,1,0:T(8,128)S(1)} custom-call(f32[2,72,256]{2,1,0:T(8,128)S(1)} %gram.1.grams, f32[64,128]{1,0:T(8,128)S(1)} %bitcast.13, f32[72,64]{1,0:T(8,128)S(1)} %collective-permute-done.5.edge), custom_call_target="tpu_custom_call" | custom-call | tf_op jit(solution)/shard_map/transform/pallas_call | solution.py:392
  67.2 0.0 collective-permute-done.2.refs_1_
  67.2 0.0 collective-permute-done.3.refs_2_
  67.2 0.0 collective-permute-done.4.refs_3_
  67.2 0.9 apply.1
  68.2 1.0 %collective-permute-start.6 = (f32[2,16,4096]{2,1,0:T(8,128)S(1)}, f32[2,16,4096]{2,1,0:T(8,128)S(1)}, u32[]{:S(2)}, u32[]{:S(2)}) collective-permute-start(f32[2,16,4096]{2,1,0:T(8,128)S(1)} %get-tuple-element.33), channel_id=1, source_target_pairs={{0,192},{64,0},{128,64},{192,128},{1,193},{65,1},{129,65},{193,129... | collective-permute-start | bytes 1572872 | tf_op jit(solution)/shard_map/ppermute | solution.py:374
  69.1 1.8 %collective-permute-start.7 = (f32[2,16,4096]{2,1,0:T(8,128)S(1)}, f32[2,16,4096]{2,1,0:T(8,128)S(1)}, u32[]{:S(2)}, u32[]{:S(2)}) collective-permute-start(f32[2,16,4096]{2,1,0:T(8,128)S(1)} %get-tuple-element.34), channel_id=1, source_target_pairs={{0,128},{64,192},{128,0},{192,64},{1,129},{65,193},{129,1},{193,65... | collective-permute-start | bytes 1572872 | tf_op jit(solution)/shard_map/ppermute | solution.py:374
  70.9 0.6 collective-permute-start.8
  71.5 9.5 %collective-permute-done.6.refs_1_ = f32[2,16,4096]{2,1,0:T(8,128)S(1)} collective-permute-done((f32[2,16,4096]{2,1,0:T(8,128)S(1)}, f32[2,16,4096]{2,1,0:T(8,128)S(1)}, u32[]{:S(2)}, u32[]{:S(2)}) %collective-permute-start.6) | collective-permute-done | bytes 524320 | tf_op jit(solution)/shard_map/ppermute | solution.py:374
  81.1 2.2 %collective-permute-done.7.refs_2_ = f32[2,16,4096]{2,1,0:T(8,128)S(1)} collective-permute-done((f32[2,16,4096]{2,1,0:T(8,128)S(1)}, f32[2,16,4096]{2,1,0:T(8,128)S(1)}, u32[]{:S(2)}, u32[]{:S(2)}) %collective-permute-start.7) | collective-permute-done | bytes 524320 | tf_op jit(solution)/shard_map/ppermute | solution.py:374
  83.2 12.5 %collective-permute-done.8.refs_3_ = f32[2,16,4096]{2,1,0:T(8,128)S(1)} collective-permute-done((f32[2,16,4096]{2,1,0:T(8,128)S(1)}, f32[2,16,4096]{2,1,0:T(8,128)S(1)}, u32[]{:S(2)}, u32[]{:S(2)}) %collective-permute-start.8) | collective-permute-done | bytes 524320 | tf_op jit(solution)/shard_map/ppermute | solution.py:374
  95.7 1.4 %assemble.1 = (f32[16,16384]{1,0:T(8,128)}, f32[16,16384]{1,0:T(8,128)}) custom-call(f32[2,16,4096]{2,1,0:T(8,128)S(1)} %get-tuple-element.32.refs_0_, f32[2,16,4096]{2,1,0:T(8,128)S(1)} %collective-permute-done.6.refs_1_, f32[2,16,4096]{2,1,0:T(8,128)S(1)} %collective-permute-done.7.refs_2_, f32[2,16,4096]{2,1,0:T(8,128)S(1)} %collective-permute-done.8.refs_3_), custom_call_target="tpu_custom_call" | custom-call | tf_op jit(solution)/shard_map/assemble/pallas_call | solution.py:411
Async XLA Ops:
  0.6 12.0 %copy-start = (f32[16,16384]{1,0:T(8,128)S(1)}, f32[16,16384]{1,0:T(8,128)}, u32[]{:S(2)}) copy-start(f32[16,16384]{1,0:T(8,128)} %depth.1) | copy-start | bytes 3145732
  0.6 12.0 %copy-start.1 = (f32[16,16384]{1,0:T(8,128)S(1)}, f32[16,16384]{1,0:T(8,128)}, u32[]{:S(2)}) copy-start(f32[16,16384]{1,0:T(8,128)} %flow.1) | copy-start | bytes 3145732
  0.7 11.9 %copy-start.2 = (s32[2,16384]{1,0:T(2,128)S(1)}, s32[2,16384]{1,0:T(2,128)}, u32[]{:S(2)}) copy-start(s32[2,16384]{1,0:T(2,128)} %pump.1) | copy-start | bytes 393220
  0.7 11.9 %copy-start.3 = (s32[16384]{0:T(1024)S(1)}, s32[16384]{0:T(1024)}, u32[]{:S(2)}) copy-start(s32[16384]{0:T(1024)} %param.10) | copy-start | bytes 196612
  0.7 11.9 %copy-start.4 = (f32[16384]{0:T(1024)S(1)}, f32[16384]{0:T(1024)}, u32[]{:S(2)}) copy-start(f32[16384]{0:T(1024)} %param.12) | copy-start | bytes 196612
  0.7 11.9 %copy-start.7 = (f32[1,512]{1,0:T(1,128)S(1)}, f32[1,512]{1,0:T(1,128)}, u32[]{:S(2)}) copy-start(f32[1,512]{1,0:T(1,128)} %error.1) | copy-start | bytes 6148
  2.2 10.4 %copy-start.6 = (f32[1,512]{1,0:T(1,128)S(1)}, f32[1,512]{1,0:T(1,128)}, u32[]{:S(2)}) copy-start(f32[1,512]{1,0:T(1,128)} %value.1) | copy-start | bytes 6148
  2.2 10.4 %copy-start.5 = (s32[1,512]{1,0:T(1,128)S(1)}, s32[1,512]{1,0:T(1,128)}, u32[]{:S(2)}) copy-start(s32[1,512]{1,0:T(1,128)} %offsets.3) | copy-start | bytes 6148
  2.2 7.0 %collective-permute-start = (f32[40,128]{1,0:T(8,128)}, f32[40,128]{1,0:T(8,128)S(1)}, u32[]{:S(2)}, u32[]{:S(2)}) collective-permute-start(f32[40,128]{1,0:T(8,128)} %get-tuple-element.19), channel_id=1, source_target_pairs={{0,1},{1,2},{2,3},{3,4},{4,5},{5,6},{6,7},{7,8},{8,9},{9,10},{10,1... | collective-permute-start | bytes 61448 | tf_op jit(solution)/shard_map/ppermute | solution.py:344
  7.3 5.3 %collective-permute-start.1 = (f32[40,128]{1,0:T(8,128)}, f32[40,128]{1,0:T(8,128)S(1)}, u32[]{:S(2)}, u32[]{:S(2)}) collective-permute-start(f32[40,128]{1,0:T(8,128)} %get-tuple-element.20), channel_id=1, source_target_pairs={{1,0},{2,1},{3,2},{4,3},{5,4},{6,5},{7,6},{8,7},{9,8},{10,9},{11,1... | collective-permute-start | bytes 61448 | tf_op jit(solution)/shard_map/ppermute | solution.py:345
  31.4 35.7 %collective-permute-start.2 = (f32[2,16,4096]{2,1,0:T(8,128)S(1)}, f32[2,16,4096]{2,1,0:T(8,128)S(1)}, u32[]{:S(2)}, u32[]{:S(2)}) collective-permute-start(f32[2,16,4096]{2,1,0:T(8,128)S(1)} %get-tuple-element.27), channel_id=1, source_target_pairs={{0,64},{64,128},{128,192},{192,0},{1,65},{65,129},{129,193},{193,1... | collective-permute-start | bytes 1572872 | tf_op jit(solution)/shard_map/ppermute | solution.py:374
  31.7 35.5 %collective-permute-start.3 = (f32[2,16,4096]{2,1,0:T(8,128)}, f32[2,16,4096]{2,1,0:T(8,128)S(1)}, u32[]{:S(2)}, u32[]{:S(2)}) collective-permute-start(f32[2,16,4096]{2,1,0:T(8,128)} %get-tuple-element.28), channel_id=1, source_target_pairs={{0,128},{64,192},{128,0},{192,64},{1,129},{65,193},{129,1},{193,65... | collective-permute-start | bytes 1572872 | tf_op jit(solution)/shard_map/ppermute | solution.py:374
  33.5 33.7 %collective-permute-start.4 = (f32[2,16,4096]{2,1,0:T(8,128)}, f32[2,16,4096]{2,1,0:T(8,128)S(1)}, u32[]{:S(2)}, u32[]{:S(2)}) collective-permute-start(f32[2,16,4096]{2,1,0:T(8,128)} %get-tuple-element.29), channel_id=1, source_target_pairs={{0,192},{64,0},{128,64},{192,128},{1,193},{65,1},{129,65},{193,129... | collective-permute-start | bytes 1572872 | tf_op jit(solution)/shard_map/ppermute | solution.py:374
  34.1 22.7 %all-to-all-start.1 = ((f32[64,1,128]{2,1,0:T(1,128)}), f32[64,1,128]{2,1,0:T(1,128)S(1)}, u32[]{:S(2)}, u32[]{:S(2)}) async-start(f32[64,1,128]{2,1,0:T(1,128)} %bitcast.4), calls=%async_computation.1 | async-start | bytes 65536 | tf_op jit(solution)/shard_map/all_to_all | solution.py:381
  47.5 4.7 %collective-permute-start.5 = (f32[72,64]{1,0:T(8,128)S(1)}, f32[72,64]{1,0:T(8,128)S(1)}, u32[]{:S(2)}, u32[]{:S(2)}) collective-permute-start(f32[72,64]{1,0:T(8,128)S(1)} %get-tuple-element.31), channel_id=1, source_target_pairs={{0,1},{1,2},{2,3},{3,4},{4,5},{5,6},{6,7},{7,8},{8,9},{9,10},{10,1... | collective-permute-start | bytes 55304 | tf_op jit(solution)/shard_map/ppermute | solution.py:380
  68.2 12.9 %collective-permute-start.6 = (f32[2,16,4096]{2,1,0:T(8,128)S(1)}, f32[2,16,4096]{2,1,0:T(8,128)S(1)}, u32[]{:S(2)}, u32[]{:S(2)}) collective-permute-start(f32[2,16,4096]{2,1,0:T(8,128)S(1)} %get-tuple-element.33), channel_id=1, source_target_pairs={{0,192},{64,0},{128,64},{192,128},{1,193},{65,1},{129,65},{193,129... | collective-permute-start | bytes 1572872 | tf_op jit(solution)/shard_map/ppermute | solution.py:374
  69.1 14.1 %collective-permute-start.7 = (f32[2,16,4096]{2,1,0:T(8,128)S(1)}, f32[2,16,4096]{2,1,0:T(8,128)S(1)}, u32[]{:S(2)}, u32[]{:S(2)}) collective-permute-start(f32[2,16,4096]{2,1,0:T(8,128)S(1)} %get-tuple-element.34), channel_id=1, source_target_pairs={{0,128},{64,192},{128,0},{192,64},{1,129},{65,193},{129,1},{193,65... | collective-permute-start | bytes 1572872 | tf_op jit(solution)/shard_map/ppermute | solution.py:374
  70.9 24.8 %collective-permute-start.8 = (f32[2,16,4096]{2,1,0:T(8,128)S(1)}, f32[2,16,4096]{2,1,0:T(8,128)S(1)}, u32[]{:S(2)}, u32[]{:S(2)}) collective-permute-start(f32[2,16,4096]{2,1,0:T(8,128)S(1)} %get-tuple-element.35), channel_id=1, source_target_pairs={{0,64},{64,128},{128,192},{192,0},{1,65},{65,129},{129,193},{193,1... | collective-permute-start | bytes 1572872 | tf_op jit(solution)/shard_map/ppermute | solution.py:374
